TPU v7x, 64 devices: a 2x2x8 block of a 4x4x8 slice. The times are simulated.
64 devices in a mesh: dp: 4 (over x, y), cp: 16 (over z, core).
Axes of the slice: x: 2, y: 2, z: 8, core: 2. Of those that a mesh axis runs over, the one named last changes fastest.
The devices are a block of a 4x4x8 slice.
Arguments:
- x_norm: bfloat16 [4096, 2048], P(('dp', 'cp')), parts along dimension 0
- y_grad: bfloat16 [4096, 2048], P(('dp', 'cp')), parts along dimension 0
- w_q: bfloat16 [2048, 16, 192], replicated
- w_dkv: bfloat16 [2048, 512], replicated
- g_kv: bfloat16 [512], replicated
- w_kr: bfloat16 [2048, 64], replicated
- w_uk: bfloat16 [512, 16, 128], replicated
- w_uv: bfloat16 [512, 16, 128], replicated
- w_o: bfloat16 [16, 128, 2048], replicated
Outputs:
- output 1: bfloat16 [4096, 2048], P(('dp', 'cp')), parts along dimension 0
- output 2: bfloat16 [4096, 2048], P(('dp', 'cp')), parts along dimension 0
- output 3: float32 [8192, 16, 192], P('dp'), parts along dimension 0
- output 4: float32 [8192, 512], P('dp'), parts along dimension 0
- output 5: float32 [2048], P('dp'), parts along dimension 0
- output 6: float32 [8192, 64], P('dp'), parts along dimension 0
- output 7: float32 [2048, 16, 128], P('dp'), parts along dimension 0
- output 8: float32 [2048, 16, 128], P('dp'), parts along dimension 0
- output 9: float32 [64, 128, 2048], P('dp'), parts along dimension 0
There are 4 independent parts. A program takes and returns all parts, laid end to end along the dimension named above; an argument that names none is the same for every part.
All inputs are finite; a program needn't handle non-finite values.
Results may differ from a plain program's by a relative error of at most 0.0156227.
Values are sent between devices in bfloat16 or wider.
A program may use at most 768 MiB of HBM per device.

v0:
```python
import jax
import jax.numpy as jnp
from jax import lax
from jax.sharding import PartitionSpec as P

ROPE_THETA = 10000.0
NORM_EPS = 1e-6


def rope_tables(positions, rope_dim):
    half_dim = rope_dim // 2
    inv_freq = ROPE_THETA ** (-(jnp.arange(half_dim, dtype=jnp.float32) * 2.0 / rope_dim))
    angles = positions.astype(jnp.float32)[:, None] * inv_freq[None, :]
    return jnp.cos(angles), jnp.sin(angles)


def rope_apply(t_in, cos_t, sin_t):
    half_dim = t_in.shape[-1] // 2
    first_half = t_in[..., :half_dim]
    second_half = t_in[..., half_dim:]
    return jnp.concatenate([first_half * cos_t - second_half * sin_t, second_half * cos_t + first_half * sin_t], axis=-1)


def rope_back(g_in, cos_t, sin_t):
    half_dim = g_in.shape[-1] // 2
    first_half = g_in[..., :half_dim]
    second_half = g_in[..., half_dim:]
    return jnp.concatenate([first_half * cos_t + second_half * sin_t, second_half * cos_t - first_half * sin_t], axis=-1)


def project_local(x_loc, w_q, w_dkv, g_kv, w_kr, cos_t, sin_t):
    nope_dim = w_q.shape[2] - w_kr.shape[1]
    q_full = jnp.einsum('td,dhe->the', x_loc, w_q, preferred_element_type=jnp.float32)
    q_nope = q_full[..., :nope_dim].astype(jnp.bfloat16)
    q_rope = rope_apply(q_full[..., nope_dim:], cos_t[:, None, :], sin_t[:, None, :]).astype(jnp.bfloat16)
    c_raw = jnp.dot(x_loc, w_dkv, preferred_element_type=jnp.float32)
    inv_rms = lax.rsqrt(jnp.mean(c_raw * c_raw, axis=-1, keepdims=True) + NORM_EPS)
    c_norm = c_raw * inv_rms
    latent = (c_norm * g_kv.astype(jnp.float32)).astype(jnp.bfloat16)
    k_rope = rope_apply(jnp.dot(x_loc, w_kr, preferred_element_type=jnp.float32), cos_t, sin_t).astype(jnp.bfloat16)
    return q_nope, q_rope, c_norm, inv_rms, latent, k_rope


def project_back(x_loc, w_q, w_dkv, g_kv, w_kr, cos_t, sin_t, dq_nope, dq_rope, d_latent, dk_rope, c_norm, inv_rms):
    dq_full = jnp.concatenate([dq_nope, rope_back(dq_rope, cos_t[:, None, :], sin_t[:, None, :])], axis=-1).astype(jnp.bfloat16)
    d_norm = d_latent * g_kv.astype(jnp.float32)
    gg_kv = jnp.sum(d_latent * c_norm, axis=0)
    dc_raw = (inv_rms * (d_norm - c_norm * jnp.mean(d_norm * c_norm, axis=-1, keepdims=True))).astype(jnp.bfloat16)
    dkr_raw = rope_back(dk_rope, cos_t, sin_t).astype(jnp.bfloat16)
    gw_q = jnp.einsum('td,the->dhe', x_loc, dq_full, preferred_element_type=jnp.float32)
    gw_dkv = jnp.einsum('td,tc->dc', x_loc, dc_raw, preferred_element_type=jnp.float32)
    gw_kr = jnp.einsum('td,tr->dr', x_loc, dkr_raw, preferred_element_type=jnp.float32)
    dx_loc = (jnp.einsum('the,dhe->td', dq_full, w_q, preferred_element_type=jnp.float32) + jnp.einsum('tc,dc->td', dc_raw, w_dkv, preferred_element_type=jnp.float32) + jnp.einsum('tr,dr->td', dkr_raw, w_kr, preferred_element_type=jnp.float32))
    return dx_loc, gw_q, gw_dkv, gg_kv, gw_kr


def key_mask(my_idx, blk_idx, chunk_len):
    q_pos = my_idx * chunk_len + jnp.arange(chunk_len)
    k_pos = blk_idx * chunk_len + jnp.arange(chunk_len)
    return (q_pos[:, None] >= k_pos[None, :])[None]


def block_scores(q_nope, q_rope, k_nope, k_rope, mask_blk, attn_scale):
    scores = (jnp.einsum('qhn,khn->hqk', q_nope, k_nope, preferred_element_type=jnp.float32) + jnp.einsum('qhr,kr->hqk', q_rope, k_rope, preferred_element_type=jnp.float32)) * attn_scale
    return jnp.where(mask_blk, scores, -jnp.inf)


def add_rows(buffer, block, row_start):
    current = lax.dynamic_slice_in_dim(buffer, row_start, block.shape[0], 0)
    return lax.dynamic_update_slice_in_dim(buffer, current + block, row_start, 0)


def attend_forward(q_nope, q_rope, k_nope_all, k_rope_all, v_all, my_idx, attn_scale):
    chunk_len = q_nope.shape[0]
    num_heads = q_nope.shape[1]
    v_dim = v_all.shape[2]

    def fwd_step(blk_idx, loop_state):
        run_max, run_sum, acc_out = loop_state
        blk_start = blk_idx * chunk_len
        k_nope = lax.dynamic_slice_in_dim(k_nope_all, blk_start, chunk_len, 0)
        k_rope = lax.dynamic_slice_in_dim(k_rope_all, blk_start, chunk_len, 0)
        v_blk = lax.dynamic_slice_in_dim(v_all, blk_start, chunk_len, 0)
        scores = block_scores(q_nope, q_rope, k_nope, k_rope, key_mask(my_idx, blk_idx, chunk_len), attn_scale)
        new_max = jnp.maximum(run_max, jnp.max(scores, axis=-1))
        rescale = jnp.exp(run_max - new_max)
        prob = jnp.exp(scores - new_max[..., None])
        run_sum = run_sum * rescale + jnp.sum(prob, axis=-1)
        acc_out = acc_out * rescale[..., None] + jnp.einsum('hqk,khv->hqv', prob.astype(jnp.bfloat16), v_blk, preferred_element_type=jnp.float32)
        return new_max, run_sum, acc_out

    init_state = (jnp.full((num_heads, chunk_len), -jnp.inf, jnp.float32), jnp.zeros((num_heads, chunk_len), jnp.float32), jnp.zeros((num_heads, chunk_len, v_dim), jnp.float32))
    run_max, run_sum, acc_out = lax.fori_loop(0, my_idx + 1, fwd_step, init_state)
    return acc_out / run_sum[..., None], run_max + jnp.log(run_sum)


def attend_backward(q_nope, q_rope, k_nope_all, k_rope_all, v_all, d_out, log_sum, row_dot, my_idx, attn_scale):
    chunk_len = q_nope.shape[0]

    def bwd_step(blk_idx, loop_state):
        dq_nope, dq_rope, dk_nope_all, dk_rope_all, dv_all = loop_state
        blk_start = blk_idx * chunk_len
        k_nope = lax.dynamic_slice_in_dim(k_nope_all, blk_start, chunk_len, 0)
        k_rope = lax.dynamic_slice_in_dim(k_rope_all, blk_start, chunk_len, 0)
        v_blk = lax.dynamic_slice_in_dim(v_all, blk_start, chunk_len, 0)
        scores = block_scores(q_nope, q_rope, k_nope, k_rope, key_mask(my_idx, blk_idx, chunk_len), attn_scale)
        prob = jnp.exp(scores - log_sum[..., None])
        dv_blk = jnp.einsum('hqk,hqv->khv', prob.astype(jnp.bfloat16), d_out, preferred_element_type=jnp.float32)
        d_prob = jnp.einsum('hqv,khv->hqk', d_out, v_blk, preferred_element_type=jnp.float32)
        d_score = (prob * (d_prob - row_dot[..., None]) * attn_scale).astype(jnp.bfloat16)
        dq_nope = dq_nope + jnp.einsum('hqk,khn->qhn', d_score, k_nope, preferred_element_type=jnp.float32)
        dq_rope = dq_rope + jnp.einsum('hqk,kr->qhr', d_score, k_rope, preferred_element_type=jnp.float32)
        dk_blk = jnp.einsum('hqk,qhn->khn', d_score, q_nope, preferred_element_type=jnp.float32)
        dkr_blk = jnp.einsum('hqk,qhr->kr', d_score, q_rope, preferred_element_type=jnp.float32)
        dk_nope_all = add_rows(dk_nope_all, dk_blk, blk_start)
        dk_rope_all = add_rows(dk_rope_all, dkr_blk, blk_start)
        dv_all = add_rows(dv_all, dv_blk, blk_start)
        return dq_nope, dq_rope, dk_nope_all, dk_rope_all, dv_all

    init_state = (jnp.zeros(q_nope.shape, jnp.float32), jnp.zeros(q_rope.shape, jnp.float32), jnp.zeros(k_nope_all.shape, jnp.float32), jnp.zeros(k_rope_all.shape, jnp.float32), jnp.zeros(v_all.shape, jnp.float32))
    return lax.fori_loop(0, my_idx + 1, bwd_step, init_state)


def solution(mesh):
    row_spec = P(('dp', 'cp'), None)
    in_specs = (row_spec, row_spec, P(), P(), P(), P(), P(), P(), P())
    out_specs = (row_spec, row_spec, P('dp', None, None), P('dp', None), P('dp'), P('dp', None), P('dp', None, None), P('dp', None, None), P('dp', None, None))

    def device_fn(x_loc, gy_loc, w_q, w_dkv, g_kv, w_kr, w_uk, w_uv, w_o):
        chunk_len = x_loc.shape[0]
        attn_scale = w_q.shape[2] ** -0.5
        my_idx = lax.axis_index('cp')
        cos_t, sin_t = rope_tables(my_idx * chunk_len + jnp.arange(chunk_len), w_kr.shape[1])
        q_nope, q_rope, c_norm, inv_rms, latent, k_rope = project_local(x_loc, w_q, w_dkv, g_kv, w_kr, cos_t, sin_t)
        k_nope = jnp.einsum('tc,chn->thn', latent, w_uk, preferred_element_type=jnp.float32).astype(jnp.bfloat16)
        v_loc = jnp.einsum('tc,chv->thv', latent, w_uv, preferred_element_type=jnp.float32).astype(jnp.bfloat16)
        k_nope_all = lax.all_gather(k_nope, 'cp', axis=0, tiled=True)
        k_rope_all = lax.all_gather(k_rope, 'cp', axis=0, tiled=True)
        v_all = lax.all_gather(v_loc, 'cp', axis=0, tiled=True)
        attn_out, log_sum = attend_forward(q_nope, q_rope, k_nope_all, k_rope_all, v_all, my_idx, attn_scale)
        attn_bf16 = attn_out.astype(jnp.bfloat16)
        y_loc = jnp.einsum('hqv,hvd->qd', attn_bf16, w_o, preferred_element_type=jnp.float32).astype(jnp.bfloat16)
        d_out = jnp.einsum('qd,hvd->hqv', gy_loc, w_o, preferred_element_type=jnp.float32).astype(jnp.bfloat16)
        gw_o = jnp.einsum('hqv,qd->hvd', attn_bf16, gy_loc, preferred_element_type=jnp.float32)
        row_dot = jnp.sum(d_out.astype(jnp.float32) * attn_out, axis=-1)
        dq_nope, dq_rope, dk_nope_all, dk_rope_all, dv_all = attend_backward(q_nope, q_rope, k_nope_all, k_rope_all, v_all, d_out, log_sum, row_dot, my_idx, attn_scale)
        dk_nope = lax.psum_scatter(dk_nope_all, 'cp', scatter_dimension=0, tiled=True).astype(jnp.bfloat16)
        dk_rope = lax.psum_scatter(dk_rope_all, 'cp', scatter_dimension=0, tiled=True)
        dv_loc = lax.psum_scatter(dv_all, 'cp', scatter_dimension=0, tiled=True).astype(jnp.bfloat16)
        gw_uk = jnp.einsum('tc,thn->chn', latent, dk_nope, preferred_element_type=jnp.float32)
        gw_uv = jnp.einsum('tc,thv->chv', latent, dv_loc, preferred_element_type=jnp.float32)
        d_latent = jnp.einsum('thn,chn->tc', dk_nope, w_uk, preferred_element_type=jnp.float32) + jnp.einsum('thv,chv->tc', dv_loc, w_uv, preferred_element_type=jnp.float32)
        dx_loc, gw_q, gw_dkv, gg_kv, gw_kr = project_back(x_loc, w_q, w_dkv, g_kv, w_kr, cos_t, sin_t, dq_nope, dq_rope, d_latent, dk_rope, c_norm, inv_rms)
        weight_grads = lax.psum((gw_q, gw_dkv, gg_kv, gw_kr, gw_uk, gw_uv, gw_o), 'cp')
        return (y_loc, dx_loc.astype(jnp.bfloat16)) + tuple(weight_grads)

    return jax.shard_map(device_fn, mesh=mesh, in_specs=in_specs, out_specs=out_specs, check_vma=False)
```

profile of v0, /device:TPU:21, one launch (start us, length us, event | category | flops | bytes accessed | tf_op | source)
XLA Modules:
  0.0 1225.4 jit_solution(8545073936872907350)
XLA Ops:
  8.1 2.3 multiply_reduce_fusion.3
  12.5 2.8 fusion.53
  16.2 8.7 fusion.73
  25.6 24.4 %all_gather.10 = bf16[1024,64]{1,0:T(8,128)(2,1)} all-gather(bf16[64,64]{1,0:T(8,128)(2,1)S(1)} %copy.45), channel_id=1, replica_groups=mesh['dp'=4,'cp'=16] {'cp'}, dimensions={0}, use_global_device_ids=true | all-gather | bytes 139264 | tf_op jit(solution)/shard_map/all_gather | solution.py:138
  50.0 6.3 all-gather.5.cloned.1.call-done
  56.3 39.8 %all-gather.3.cloned.1.call-done = bf16[1024,16,128]{2,0,1:T(8,128)(2,1)} async-done(((bf16[64,16,128]{2,0,1:T(8,128)(2,1)}), bf16[1024,16,128]{2,0,1:T(8,128)(2,1)}) %all-gather.3.cloned.1.call-update) | async-done | bytes 4194320 | tf_op jit(solution)/shard_map/all_gather | solution.py:137
  96.2 7.9 while.36
  96.3 1.2 convolution_bitcast_fusion.16
  98.8 1.4 convolution_add_fusion.4
  102.8 1.4 convolution_add_fusion.4
  104.2 6.9 multiply_reduce_fusion
  113.6 4.1 broadcast.154.clone
  117.7 4.2 broadcast.154
  121.9 27.7 %while.37 = (s32[]{:T(128)}, f32[64,16,128]{2,0,1:T(8,128)}, f32[64,16,64]{0,2,1:T(8,128)}, f32[1024,16,128]{2,0,1:T(8,128)}, f32[1024,64]{1,0:T(8,128)}, /*inde...) while((s32[]{:T(128)}, f32[64,16,128]{2,0,1:T(8,128)}, ...), condition=%wide.region_7.8_spmd, body=%wide.region_6.7_spmd.sunk | while | flops 110108800 | bytes 8226063 | solution.py:121
  125.0 1.3 fusion.192
  127.3 2.1 fusion.194
  129.4 2.2 fusion.193
  131.6 2.1 fusion.197
  133.7 2.0 fusion.195
  138.9 1.3 fusion.192
  141.1 2.1 fusion.194
  143.2 2.2 fusion.193
  145.4 2.1 fusion.197
  147.5 2.0 fusion.195
  153.3 1.5 add_convert_fusion
  154.8 9.9 fusion.69
  164.7 10.8 convolution_bitcast_fusion.9
  175.5 272.1 %reduce-scatter.10.cloned.1.call-done = f32[64,64]{1,0:T(8,128)} async-done(((f32[1024,64]{1,0:T(8,128)}), f32[64,64]{1,0:T(8,128)}) %reduce-scatter.10.cloned.1.call-update) | async-done | bytes 16400
  447.6 1.5 fusion.106
  449.1 1.4 copy.70
  450.5 1.4 copy.69
  454.5 61.3 %reduce-scatter.6.cloned.1.call-done = f32[64,16,128]{2,0,1:T(8,128)} async-done(((f32[1024,16,128]{2,0,1:T(8,128)}), f32[64,16,128]{2,0,1:T(8,128)}) %reduce-scatter.6.cloned.1.call-update) | async-done | bytes 524304 | tf_op jit(solution)/shard_map/reduce_scatter | solution.py:147
  515.8 3.2 fusion.60
  519.0 65.2 %reduce-scatter.8.cloned.1.call-done = f32[64,16,128]{2,0,1:T(8,128)} async-done(((f32[1024,16,128]{2,0,1:T(8,128)}), f32[64,16,128]{2,0,1:T(8,128)}) %reduce-scatter.8.cloned.1.call-update) | async-done | bytes 524304 | tf_op jit(solution)/shard_map/reduce_scatter | solution.py:149
  584.2 2.5 multiply_reduce_fusion.1
  587.5 2.7 convolution_bitcast_fusion.10
  590.3 2.7 fusion.76
  593.0 2.7 fusion.79
  595.9 5.8 fusion.44
  601.6 7.1 convolution_bitcast_fusion.13
  608.8 27.6 %psum.51 = f32[512]{0:T(512)} all-reduce(f32[512]{0:T(512)S(1)} %copy-done.26), channel_id=1, replica_groups=mesh['dp'=4,'cp'=16] {'cp'}, use_global_device_ids=true, to_apply=%region_15.16 | all-reduce | flops 512 | bytes 4096 | tf_op jit(solution)/shard_map/psum | solution.py:154
  637.2 1.9 fusion.43
  639.1 536.2 %all-reduce.3.cloned.1.call-done = (f32[2048,16,192]{0,2,1:T(8,128)}, f32[2048,512]{0,1:T(8,128)}, f32[2048,64]{0,1:T(8,128)}, f32[512,16,128]{2,0,1:T(8,128)}, ...) async-done(((f32[2048,16,192]{0,2,1:T(8,128)}, f32[2048,512]{0,1:T(8,128)}, f32[2048,64]{0,1:T(8,128)}, f32[512,16,128]{2,0,1:T(8,128)}, f32[512,16,128]{2,0,1:T(8,128)}, ...) | async-done | bytes 55050256 | tf_op jit(solution)/shard_map/psum | solution.py:154
  1175.2 5.3 copy.54
  1180.6 6.8 copy.55
  1187.4 4.4 copy.56
  1191.8 19.7 %copy.138 = f32[2048,16,192]{0,2,1:T(8,128)} copy(f32[2048,16,192]{0,2,1:T(8,128)} %get-tuple-element.777) | data formatting | bytes 50331648
  1212.3 6.3 copy.140
  (145 shorter events, 27.5 us)
Async XLA Ops:
  7.2 4.0 copy-start
  7.2 8.3 copy-start.5
  7.2 8.3 copy-start.15
  7.2 49.1 %all-gather.5.cloned.1.call-start = ((), (), s32[]{:S(2)}) async-start(), calls=%async_computation.4 | async-start | bytes 4456448 | tf_op jit(solution)/shard_map/all_gather | solution.py:139
  8.1 2.3 copy-start.25
  10.4 0.7 copy-start.13
  10.4 0.6 copy-start.27
  11.2 13.7 %copy-start.16 = (bf16[64,512,1]{1,0,2:T(8,128)(2,1)}, bf16[64,512,1]{1,0,2:T(8,128)(2,1)S(1)}, u32[]{:S(2)}) copy-start(bf16[64,512,1]{1,0,2:T(8,128)(2,1)S(1)} %fusion.82) | copy-start | bytes 196612
  12.5 83.7 %all-gather.3.cloned.1.call-start = ((), (), s32[]{:S(2)}) async-start(), calls=%async_computation.3 | async-start | bytes 4456448 | tf_op jit(solution)/shard_map/all_gather | solution.py:137
  15.4 432.2 %reduce-scatter.10.cloned.1.call-start = ((), (), s32[]{:S(2)}) async-start(), calls=%async_computation.7 | async-start | bytes 557056
  15.5 9.4 copy-start.28
  15.5 9.4 copy-start.29
  16.2 8.8 copy-start.21
  104.1 7.0 copy-start.2
  149.7 366.1 %reduce-scatter.6.cloned.1.call-start = ((), (), s32[]{:S(2)}) async-start(), calls=%async_computation.5 | async-start | bytes 8912896 | tf_op jit(solution)/shard_map/reduce_scatter | solution.py:147
  150.3 433.9 %reduce-scatter.8.cloned.1.call-start = ((), (), s32[]{:S(2)}) async-start(), calls=%async_computation.6 | async-start | bytes 8912896 | tf_op jit(solution)/shard_map/reduce_scatter | solution.py:149
  150.4 1.9 copy-start.4
  150.4 2.9 copy-start.22
  150.4 4.4 copy-start.3
  150.9 1024.3 %all-reduce.3.cloned.1.call-start = ((), (), s32[]{:S(2)}) async-start(), calls=%async_computation.8 | async-start | bytes 110100480 | tf_op jit(solution)/shard_map/psum | solution.py:154
  154.8 9.9 copy-start.9
  154.8 9.9 copy-start.6
  164.7 419.6 %copy-start.14 = (f32[64,512]{1,0:T(8,128)S(1)}, f32[64,512]{1,0:T(8,128)}, u32[]{:S(2)}) copy-start(f32[64,512]{1,0:T(8,128)} %copy-done.13) | copy-start | bytes 393220
  452.9 0.6 copy-start.23
  584.2 6.1 copy-start.12
  584.2 6.1 copy-start.17
  587.5 5.5 copy-start.18
  587.5 5.5 copy-start.11
  595.8 5.8 copy-start.10
  601.6 7.1 copy-start.26
  601.6 34.8 %copy-start.7 = (bf16[2048,512]{1,0:T(8,128)(2,1)S(1)}, bf16[2048,512]{1,0:T(8,128)(2,1)}, u32[]{:S(2)}) copy-start(bf16[2048,512]{1,0:T(8,128)(2,1)} %param.16) | copy-start | bytes 6291460
  601.6 34.8 %copy-start.19 = (bf16[64,512]{1,0:T(8,128)(2,1)S(1)}, bf16[64,512]{1,0:T(8,128)(2,1)}, u32[]{:S(2)}) copy-start(bf16[64,512]{1,0:T(8,128)(2,1)} %copy-done.18) | copy-start | bytes 196612
  601.6 35.5 %copy-start.24 = (bf16[64,32]{0,1:T(8,128)(2,1)S(1)}, bf16[64,32]{0,1:T(8,128)(2,1)}, u32[]{:S(2)}) copy-start(bf16[64,32]{0,1:T(8,128)(2,1)} %copy-done.23) | copy-start | bytes 12292
  1180.6 6.8 copy-start.8
  1187.4 24.9 %slice-start = ((s8[16777216]{0:T(1024)(128)(4,1)}), s8[4194304]{0:T(1024)(128)(4,1)S(1)}, s32[]{:S(2)}) async-start(s8[16777216]{0:T(1024)(128)(4,1)} %bitcast.180), calls=%async_computation.9 | async-start | bytes 8388608
  1191.8 19.7 %copy-start.20 = (f32[2048,64]{0,1:T(8,128)S(1)}, f32[2048,64]{0,1:T(8,128)}, u32[]{:S(2)}) copy-start(f32[2048,64]{0,1:T(8,128)} %get-tuple-element.780) | copy-start | bytes 1572868
  1191.8 20.5 %slice-start.1 = ((s8[16777216]{0:T(1024)(128)(4,1)}), s8[4194304]{0:T(1024)(128)(4,1)S(1)}, s32[]{:S(2)}) async-start(s8[16777216]{0:T(1024)(128)(4,1)} %bitcast.180), calls=%async_computation.10 | async-start | bytes 8388608
  1191.8 20.5 %slice-start.2 = ((s8[16777216]{0:T(1024)(128)(4,1)}), s8[4194304]{0:T(1024)(128)(4,1)S(1)}, s32[]{:S(2)}) async-start(s8[16777216]{0:T(1024)(128)(4,1)} %bitcast.180), calls=%async_computation.11 | async-start | bytes 8388608
  1191.8 20.5 %slice-start.3 = ((s8[16777216]{0:T(1024)(128)(4,1)}), s8[4194304]{0:T(1024)(128)(4,1)S(1)}, s32[]{:S(2)}) async-start(s8[16777216]{0:T(1024)(128)(4,1)} %bitcast.180), calls=%async_computation.12 | async-start | bytes 8388608
  1212.3 6.3 copy-start.1
Sparse Core Ops, SparseCore 0:
  12.6 43.6 all-gather.4
  58.5 37.5 all-gather.2
  149.8 297.7 reduce-scatter.9
  449.8 65.9 reduce-scatter.5
  518.0 66.1 reduce-scatter.7
  596.0 579.2 all-reduce.2
where the time goes:
time: 1230 us
  waiting for transfers between devices  982 us (80%)
  matrix products  105 us (9%)
  local copies, waits for them, and re-layouts  64.5 us (5%)
  blocking collectives  52 us (4%)
  between operations  14.6 us (1%)
    psum x1, waiting for transfers between devices, device_fn(): lax.psum((gw_q, gw_dkv, gg_kv, gw_kr, gw_uk, gw_uv, gw_o), 'cp')  536 us
    unnamed x7, waiting for transfers between devices  273 us
    reduce_scatter x1, waiting for transfers between devices, device_fn(): lax.psum_scatter(dv_all, 'cp', scatter_dimension=0, tiled=True)  65.2 us
    reduce_scatter x1, waiting for transfers between devices, device_fn(): lax.psum_scatter(dk_nope_all, 'cp', scatter_dimension=0, tiled=True)  61.3 us
    unnamed x76, local copies, waits for them, and re-layouts  47.5 us
    all_gather x1, waiting for transfers between devices, device_fn(): k_nope_all = lax.all_gather(k_nope, 'cp', axis=0, tiled=True)  39.8 us
    psum x1, blocking collectives, device_fn(): lax.psum((gw_q, gw_dkv, gg_kv, gw_kr, gw_uk, gw_uv, gw_o), 'cp')  27.6 us
  transfers between devices with their start and end apart: 6, of which 6 were waited for; matrix products, arithmetic and copies ran while one was open for 5% of the time, Pallas kernels for 0%

commit v1 on v0

v1 whole, which is shorter than its diff:
```python
import functools

import jax
import jax.numpy as jnp
import numpy as np
from jax import lax
from jax.experimental import pallas as pl
from jax.experimental.pallas import tpu as pltpu
from jax.sharding import PartitionSpec as P

ROPE_THETA = 10000.0
NORM_EPS = 1e-6
QBLK = 256
MASKED = -1e30
LANES = 128
F32 = jnp.float32
BF16 = jnp.bfloat16
NN = (((1,), (0,)), ((), ()))
NT = (((1,), (1,)), ((), ()))
TN = (((0,), (0,)), ((), ()))


def mm(lhs, rhs, dims=NN):
    return lax.dot_general(lhs, rhs, dims, preferred_element_type=F32)


def swap_halves(t, half):
    return pltpu.roll(t, half, 1) + pltpu.roll(t, LANES - half, 1)


def block_kernel(n_chips, qk, scale, x_ref, gy_ref, tab_ref, wq_ref, wdkv_ref, gkv_ref, wkr_ref, wuk_ref, wuv_ref, wo_ref,
                 x_out, gy_out, lat_out, c_out, ot_out, dqt_out, dk_out, dv_out, dkr_out, y_out, dx_out,
                 x_s, gy_s, tab_s, tabt_s, wq_s, wdkv_s, wkr_s, wkv_raw, wkv_f32, wkv_s, wo_s, q_s, lat_s, c_s, kr_s, krt_s,
                 kn_s, v_s, kt_s, vt_s, lse_s, ot_st, do_s, dot_s, dk_acc, dv_acc, dkr_acc, y_acc, dx_acc, y_buf, dx_buf,
                 dqt_st, dk_st, dv_st,
                 ring_send, ring_recv, pr_send, pr_recv, w_sem, wq_sem, wo_sem, out_sem, loc_sem, snd_sem, rcv_sem, kr_sem, yx_sem):
    me = lax.axis_index('cp')
    core = lax.rem(me, 2)
    chip = lax.div(me, 2)
    partner = me + 1 - 2 * core
    ring_dev = (lax.rem(chip + 1, n_chips) * 2 + core, lax.rem(chip + n_chips - 1, n_chips) * 2 + core)
    rows = x_ref.shape[0]
    part = rows // 2
    both = 2 * rows
    seq = x_s.shape[0]
    heads = wq_s.shape[0]
    n_pairs = heads // 2
    nope = LANES
    rope_dim = wkr_ref.shape[0]
    half = rope_dim // 2
    far = n_chips // 2
    mesh_id = pl.DeviceIdType.MESH
    srcs, bufs = (x_ref, gy_ref), (x_s, gy_s)

    def origin(d, h):
        return lax.rem(chip + (n_chips - h if d == 0 else h), n_chips)

    def piece(arr, chip_of, core_of, p):
        start = pl.multiple_of((chip_of * 2 + core_of) * rows + p * part, part)
        return bufs[arr].at[pl.ds(start, part), :]

    def ring(arr, d, h, p, first=False):
        dst = piece(arr, origin(d, h), core, p)
        src = srcs[arr].at[pl.ds(p * part, part), :] if first else dst
        return pltpu.make_async_remote_copy(src_ref=src, dst_ref=dst, send_sem=ring_send.at[arr, d, h, p], recv_sem=ring_recv.at[arr, d, h, p], device_id={'cp': ring_dev[d]}, device_id_type=mesh_id)

    def across(arr, rel, p, first=False):
        dst = piece(arr, lax.rem(chip + n_chips - rel, n_chips), core, p)
        src = srcs[arr].at[pl.ds(p * part, part), :] if first else dst
        return pltpu.make_async_remote_copy(src_ref=src, dst_ref=dst, send_sem=pr_send.at[arr, rel, p], recv_sem=pr_recv.at[arr, rel, p], device_id={'cp': partner}, device_id_type=mesh_id)

    def hop(arr, h, p):
        for d in range(2):
            if isinstance(p, int):
                limit = far if d == p else far - 1
            else:
                limit = jnp.where(p == d, far, far - 1)

            @pl.when(h <= limit)
            def _():
                ring(arr, d, h - 1, p).wait_recv()

                @pl.when(h < limit)
                def _():
                    ring(arr, d, h, p).start()
                across(arr, h if d == 0 else n_chips - h, p).start()

    def weight_copies():
        first = core * heads
        out = [pltpu.make_async_copy(wdkv_ref, wdkv_s, w_sem.at[0]),
               pltpu.make_async_copy(wkr_ref, wkr_s.at[pl.ds(0, rope_dim), :], w_sem.at[1]),
               pltpu.make_async_copy(wuk_ref.at[:, pl.ds(pl.multiple_of(first, heads), heads), :], wkv_raw.at[0], w_sem.at[2]),
               pltpu.make_async_copy(wuv_ref.at[:, pl.ds(pl.multiple_of(first, heads), heads), :], wkv_raw.at[1], w_sem.at[3]),
               pltpu.make_async_copy(tab_ref, tab_s, w_sem.at[4])]
        for idx in range(2):
            out.append(pltpu.make_async_copy(srcs[idx], bufs[idx].at[pl.ds(pl.multiple_of(me * rows, rows), rows), :], w_sem.at[5 + idx]))
        for hh in range(heads):
            start = pl.multiple_of((first + hh) * qk, qk)
            out.append(pltpu.make_async_copy(wq_ref.at[pl.ds(start, qk), :], wq_s.at[hh, pl.ds(0, qk), :], wq_sem.at[hh]))
        return out

    def wo_copy(step):
        start = pl.multiple_of((core * n_pairs + step) * 2 * nope, 2 * nope)
        slot = lax.rem(step, 2)
        return pltpu.make_async_copy(wo_ref.at[pl.ds(start, 2 * nope), :], wo_s.at[slot], wo_sem.at[slot])

    barrier = pltpu.get_barrier_semaphore()
    for peer in (ring_dev[0], ring_dev[1], partner):
        pl.semaphore_signal(barrier, inc=1, device_id={'cp': peer}, device_id_type=mesh_id)
    for copy in weight_copies():
        copy.start()
    wo_copy(0).start()
    wo_copy(1).start()
    pl.semaphore_wait(barrier, 3)
    for p in range(2):
        for d in range(2):
            ring(0, d, 0, p, True).start()
    for arr in range(2):
        for p in range(2):
            across(arr, 0, p, True).start()

    wq_s[:, qk:, :] = jnp.zeros((heads, 2 * LANES - qk, wq_s.shape[2]), BF16)
    wkr_s[rope_dim:, :] = jnp.zeros((LANES - rope_dim, wkr_s.shape[1]), BF16)
    dkr_acc[...] = jnp.zeros_like(dkr_acc)
    y_acc[...] = jnp.zeros_like(y_acc)
    dx_acc[...] = jnp.zeros_like(dx_acc)
    for copy in weight_copies():
        copy.wait()
    tabt_s[...] = tab_s[...].T
    rank = wkv_raw.shape[1]
    for idx in range(2):
        wkv_f32[...] = wkv_raw[idx].astype(F32).reshape(rank * heads, LANES)
        for hh in range(heads):
            wkv_s[hh, :, idx * nope:(idx + 1) * nope] = wkv_f32[pl.ds(hh, rank, stride=heads), :].astype(BF16)

    lane = lax.broadcasted_iota(jnp.int32, (both, LANES), 1)

    def project(stage, starts):
        x_blk = jnp.concatenate([x_s[pl.ds(st, both), :] for st in starts], axis=0)
        cos_l, sin_l = [], []
        for st in starts:
            tab = tab_s[pl.ds(st, both), :]
            cos_l.append(jnp.where(lane < rope_dim, tab, 0.0))
            sin_l.append(jnp.where(lane < rope_dim, pltpu.roll(tab, rope_dim, 1), 0.0))
        cos_v, sin_v = jnp.concatenate(cos_l, axis=0), jnp.concatenate(sin_l, axis=0)

        def rotate(t):
            return (t * cos_v + swap_halves(t, half) * sin_v).astype(BF16)

        def put(ref, val):
            for idx, st in enumerate(starts):
                ref[pl.ds(st, both), :] = val[idx * both:(idx + 1) * both, :]

        if stage == 0:
            c_raw = mm(x_blk, wdkv_s[...])
            put(c_s, c_raw)
            inv_rms = lax.rsqrt(jnp.mean(c_raw * c_raw, axis=-1, keepdims=True) + NORM_EPS)
            put(lat_s, (c_raw * inv_rms * gkv_ref[...]).astype(BF16))
            put(kr_s, rotate(mm(x_blk, wkr_s[...], NT)))

        def head_pair(j, carry):
            for hh in range(2):
                h = stage * (heads // 2) + 2 * j + hh
                q_raw = mm(x_blk, wq_s[h], NT)
                q_val = jnp.concatenate([q_raw[:, :nope].astype(BF16), rotate(q_raw[:, nope:])], axis=1)
                for idx, st in enumerate(starts):
                    q_s[h, pl.ds(st, both), :] = q_val[idx * both:(idx + 1) * both, :]
            return carry
        lax.fori_loop(0, heads // 4, head_pair, 0)

    hop(0, 1, 0)
    hop(0, 1, 1)

    def x_stage(h, carry):
        near = h - 1
        up_rel = near
        dn_rel = jnp.where(near < far, n_chips - near, 0)
        chips = (lax.rem(chip + n_chips - up_rel, n_chips), lax.rem(chip + n_chips - dn_rel, n_chips))
        starts = [pl.multiple_of(c * both, both) for c in chips]

        @pl.when(h <= far)
        def _():
            hop(0, h, 0)

        @pl.when(h > far)
        def _():
            hop(1, 1, 0)
        for p in range(2):
            across(0, up_rel, p).wait_recv()
            across(0, dn_rel, p).wait_recv()
        project(0, starts)

        @pl.when(h <= far)
        def _():
            hop(0, h, 1)

        @pl.when(h == far - 1)
        def _():
            for p in range(2):
                for d in range(2):
                    ring(1, d, 0, p, True).start()

        @pl.when(h > far)
        def _():
            hop(1, 1, 1)
        project(1, starts)
        return carry
    lax.fori_loop(2, far + 2, x_stage, 0)

    outs = [pltpu.make_async_copy(src, dst, out_sem.at[idx]) for idx, (src, dst) in enumerate(((x_s, x_out), (lat_s, lat_out), (c_s, c_out), (gy_s, gy_out)))]
    for copy in outs[:3]:
        copy.start()
    krt_s[...] = kr_s[...].T

    row_id = lax.broadcasted_iota(jnp.int32, (QBLK, QBLK), 0)
    col_id = lax.broadcasted_iota(jnp.int32, (QBLK, QBLK), 1)
    causal = row_id <= col_id
    n_blk = seq // QBLK

    def scores(h, i):
        kl = (i + 1) * QBLK
        k_blk = jnp.concatenate([kn_s[h, :kl, :], kr_s[:kl, :]], axis=1)
        st = mm(k_blk, q_s[h, i * QBLK:kl, :], NT) * scale
        diag = jnp.where(causal, st[i * QBLK:, :], MASKED)
        return diag if i == 0 else jnp.concatenate([st[:i * QBLK, :], diag], axis=0)

    def forward(h, carry):
        @pl.when(h < 2 * (far - 1))
        def _():
            hop(1, 2 + lax.div(h, 2), lax.rem(h, 2))
        kv = mm(lat_s[...], wkv_s[h]).astype(BF16)
        kn_s[h] = kv[:, :nope]
        v_s[h] = kv[:, nope:]
        kt_s[h] = kv[:, :nope].T
        vt_s[...] = kv[:, nope:].T
        for i in range(n_blk):
            kl = (i + 1) * QBLK
            st = scores(h, i)
            top = jnp.max(st, axis=0, keepdims=True)
            pt = jnp.exp(st - top)
            total = jnp.sum(pt, axis=0, keepdims=True)
            ot = mm(vt_s[:, :kl], pt.astype(BF16)) * (1.0 / total)
            ot_st[pl.ds(pl.multiple_of(h * nope, nope), nope), i * QBLK:kl] = ot.astype(BF16)
            lse_s[h, :, i * QBLK:kl] = top + jnp.log(total)
        return carry
    lax.fori_loop(0, heads, forward, 0)

    ot_dst = ot_out.at[pl.ds(pl.multiple_of(core * heads * nope, heads * nope), heads * nope), :]
    ot_local = pltpu.make_async_copy(ot_st, ot_dst, kr_sem.at[3])
    ot_remote = pltpu.make_async_remote_copy(src_ref=ot_st, dst_ref=ot_dst, send_sem=kr_sem.at[4], recv_sem=kr_sem.at[5], device_id={'cp': partner}, device_id_type=mesh_id)
    ot_local.start()
    ot_remote.start()
    for rel in range(n_chips):
        for p in range(2):
            across(1, rel, p).wait_recv()
    outs[3].start()

    def pair_copies(step):
        slot_of = lax.rem(step, 2)
        pair = core * n_pairs + step
        col = pl.ds(pl.multiple_of(pair * 2 * nope, 2 * nope), 2 * nope)
        regions = ((dqt_st.at[slot_of], dqt_out.at[pl.ds(pl.multiple_of(pair * 2 * qk, 2 * qk), 2 * qk), :]), (dk_st.at[slot_of], dk_out.at[:, col]), (dv_st.at[slot_of], dv_out.at[:, col]))
        local, remote = [], []
        for idx, (src, dst) in enumerate(regions):
            local.append(pltpu.make_async_copy(src, dst, loc_sem.at[slot_of, idx]))
            remote.append(pltpu.make_async_remote_copy(src_ref=src, dst_ref=dst, send_sem=snd_sem.at[slot_of, idx], recv_sem=rcv_sem.at[step, idx], device_id={'cp': partner}, device_id_type=mesh_id))
        return local, remote

    chip_cols = pl.ds(pl.multiple_of(chip * both, both), both)

    def backward(g, carry):
        slot = lax.rem(g, 2)

        @pl.when(g >= 2)
        def _():
            local, remote = pair_copies(g - 2)
            for copy in local:
                copy.wait()
            for copy in remote:
                copy.wait_send()
        wo_copy(g).wait()
        do_all = mm(gy_s[...], wo_s[slot], NT).astype(BF16)
        do_s[...] = do_all
        dot_s[...] = do_all.T
        for hh in range(2):
            h = 2 * g + hh
            cols = slice(hh * nope, (hh + 1) * nope)
            for i in range(n_blk):
                kl = (i + 1) * QBLK
                lo = i * QBLK
                blk = slice(lo, kl)
                pt = jnp.exp(scores(h, i) - lse_s[h, :, blk])
                dpt = mm(v_s[h, :kl, :], dot_s[cols, blk])
                pdp = pt * dpt
                row_dot = jnp.sum(pdp, axis=0, keepdims=True)
                dst = ((pdp - pt * row_dot) * scale).astype(BF16)
                dv_add = mm(pt.astype(BF16), do_s[blk, cols])
                dk_add = mm(dst, q_s[h, blk, :])
                if i:
                    dv_acc[:lo, :] += dv_add[:lo, :]
                    dk_acc[:lo, :] += dk_add[:lo, :]
                dv_acc[blk, :] = dv_add[lo:, :]
                dk_acc[blk, :] = dk_add[lo:, :]
                kt_blk = jnp.concatenate([kt_s[h, :, :kl], krt_s[:, :kl]], axis=0)
                dqt = mm(kt_blk, dst)
                r1 = dqt[nope:nope + half, :]
                r2 = dqt[nope + half:nope + rope_dim, :]
                c_t = tabt_s[:half, blk]
                s_t = tabt_s[LANES - half:, blk]
                dqt_rot = jnp.concatenate([dqt[:nope, :], r1 * c_t + r2 * s_t, r2 * c_t - r1 * s_t], axis=0)
                dqt_st[slot, hh * qk:(hh + 1) * qk, blk] = dqt_rot.astype(BF16)
            dk_st[slot, :, cols] = dk_acc[:, :nope].astype(BF16)
            dv_st[slot, :, cols] = dv_acc[...].astype(BF16)
            dkr_acc[...] += dk_acc[:, nope:]
            dx_acc[...] += mm(dqt_st[slot, hh * qk:(hh + 1) * qk, chip_cols], wq_s[h, :qk, :], TN)
        local, remote = pair_copies(g)
        for copy in local + remote:
            copy.start()
        y_acc[...] += mm(ot_st[pl.ds(pl.multiple_of(g * 2 * nope, 2 * nope), 2 * nope), chip_cols], wo_s[slot], TN)

        @pl.when(g + 2 < n_pairs)
        def _():
            wo_copy(g + 2).start()
        return carry
    lax.fori_loop(0, n_pairs, backward, 0)

    theirs = pl.ds(pl.multiple_of((1 - core) * rows, rows), rows)
    mine = pl.ds(pl.multiple_of(core * rows, rows), rows)
    sums = [pltpu.make_async_remote_copy(src_ref=acc.at[theirs, :], dst_ref=buf, send_sem=yx_sem.at[idx], recv_sem=yx_sem.at[2 + idx], device_id={'cp': partner}, device_id_type=mesh_id) for idx, (acc, buf) in enumerate(((y_acc, y_buf), (dx_acc, dx_buf)))]
    kr_local = pltpu.make_async_copy(dkr_acc, dkr_out.at[core], kr_sem.at[0])
    kr_remote = pltpu.make_async_remote_copy(src_ref=dkr_acc, dst_ref=dkr_out.at[core], send_sem=kr_sem.at[1], recv_sem=kr_sem.at[2], device_id={'cp': partner}, device_id_type=mesh_id)
    for copy in sums + [kr_local, kr_remote]:
        copy.start()
    for arr in range(2):
        for p in range(2):
            for d in range(2):
                for h in range(far if d == p else far - 1):
                    ring(arr, d, h, p, h == 0).wait_send()
            for rel in range(n_chips):
                across(arr, rel, p, rel == 0).wait_send()
    for copy in outs:
        copy.wait()
    ot_local.wait()
    ot_remote.wait()
    for step in range(n_pairs):
        local, remote = pair_copies(step)
        if step >= n_pairs - 2:
            for copy in local:
                copy.wait()
            for copy in remote:
                copy.wait_send()
        for copy in remote:
            copy.wait_recv()
    kr_local.wait()
    kr_remote.wait()
    for copy in sums:
        copy.wait()
    y_out[...] = (y_acc[mine, :] + y_buf[...]).astype(BF16)
    dx_out[...] = dx_acc[mine, :] + dx_buf[...]


def block(x_loc, gy_loc, tab, wq_rows, w_dkv, g_row, wkr_t, w_uk, w_uv, wo_rows, n_dev, qk, scale):
    rows, width = x_loc.shape
    seq = rows * n_dev
    n_chips = n_dev // 2
    rank = w_dkv.shape[1]
    nope = LANES
    n_hv = wo_rows.shape[0]
    n_feat = wq_rows.shape[0]
    heads = n_hv // nope // 2
    n_pairs = heads // 2
    far = n_chips // 2
    hbm = pl.BlockSpec(memory_space=pl.ANY)
    vmem = pl.BlockSpec(memory_space=pltpu.VMEM)
    dma = pltpu.SemaphoreType.DMA
    vm = pltpu.VMEM
    sds = jax.ShapeDtypeStruct
    scratch = [vm((seq, width), BF16), vm((seq, width), BF16), vm((seq, LANES), F32), vm((LANES, seq), F32), vm((heads, 2 * LANES, width), BF16), vm((width, rank), BF16), vm((LANES, width), BF16),
               vm((2, rank, heads, nope), BF16), vm((rank * heads, nope), F32), vm((heads, rank, 2 * nope), BF16), vm((2, 2 * nope, width), BF16),
               vm((heads, seq, 2 * LANES), BF16), vm((seq, rank), BF16), vm((seq, rank), F32), vm((seq, LANES), BF16), vm((LANES, seq), BF16),
               vm((heads, seq, nope), BF16), vm((heads, seq, nope), BF16), vm((heads, nope, seq), BF16), vm((nope, seq), BF16), vm((heads, 1, seq), F32), vm((heads * nope, seq), BF16),
               vm((seq, 2 * nope), BF16), vm((2 * nope, seq), BF16), vm((seq, 2 * LANES), F32), vm((seq, nope), F32), vm((seq, LANES), F32),
               vm((2 * rows, width), F32), vm((2 * rows, width), F32), vm((rows, width), F32), vm((rows, width), F32),
               vm((2, 2 * qk, seq), BF16), vm((2, seq, 2 * nope), BF16), vm((2, seq, 2 * nope), BF16),
               dma((2, 2, far, 2)), dma((2, 2, far, 2)), dma((2, n_chips, 2)), dma((2, n_chips, 2)), dma((7,)), dma((heads,)), dma((2,)), dma((4,)), dma((2, 3)), dma((2, 3)), dma((n_pairs, 3)), dma((6,)), dma((4,))]
    return pl.pallas_call(
        functools.partial(block_kernel, n_chips, qk, scale),
        out_shape=(sds((seq, width), BF16), sds((seq, width), BF16), sds((seq, rank), BF16), sds((seq, rank), F32), sds((n_hv, seq), BF16), sds((n_feat, seq), BF16), sds((seq, n_hv), BF16), sds((seq, n_hv), BF16), sds((2, seq, LANES), F32), sds((rows, width), BF16), sds((rows, width), F32)),
        in_specs=[hbm] * 5 + [vmem] + [hbm] * 4,
        out_specs=[hbm] * 9 + [vmem] * 2,
        scratch_shapes=scratch,
        compiler_params=pltpu.CompilerParams(collective_id=0, has_side_effects=True, vmem_limit_bytes=67043328),
        name='latent_block',
    )(x_loc, gy_loc, tab, wq_rows, w_dkv, g_row, wkr_t, w_uk, w_uv, wo_rows)


def solution(mesh):
    n_dev = mesh.shape['cp']
    row_spec = P(('dp', 'cp'), None)
    in_specs = (row_spec, row_spec, P(), P(), P(), P(), P(), P(), P())
    out_specs = (row_spec, row_spec, P('dp', None, None), P('dp', None), P('dp'), P('dp', None), P('dp', None, None), P('dp', None, None), P('dp', None, None))

    def device_fn(x_loc, gy_loc, w_q, w_dkv, g_kv, w_kr, w_uk, w_uv, w_o):
        rows, width = x_loc.shape
        seq = rows * n_dev
        heads, qk = w_q.shape[1:]
        rope_dim = w_kr.shape[1]
        rank = w_dkv.shape[1]
        nope = qk - rope_dim
        scale = qk ** -0.5
        me = lax.axis_index('cp')
        half = rope_dim // 2
        inv_freq = ROPE_THETA ** (-(np.arange(half) * 2.0 / rope_dim))
        angles = np.arange(seq)[:, None] * inv_freq[None, :]
        cos, sin = np.cos(angles).astype(np.float32), np.sin(angles).astype(np.float32)
        tab = jnp.asarray(np.concatenate([cos, cos, -sin, sin], axis=1))

        wq_rows = jnp.transpose(w_q, (1, 2, 0)).reshape(heads * qk, width)
        wo_rows = w_o.reshape(heads * nope, width)
        wuk_cols = w_uk.reshape(rank, heads * nope)
        wuv_cols = w_uv.reshape(rank, heads * nope)
        g_f32 = g_kv.astype(F32)
        x_all, gy_all, latent, c_raw, o_t, dq_t, dk, dv, dkr, y_loc, dx_q = block(x_loc, gy_loc, tab, wq_rows, w_dkv, g_f32[None, :], w_kr.T, w_uk, w_uv, wo_rows, n_dev, qk, scale)
        inv_rms = lax.rsqrt(jnp.mean(c_raw * c_raw, axis=-1, keepdims=True) + NORM_EPS)
        c_norm = c_raw * inv_rms

        own = lambda t: lax.dynamic_slice_in_dim(t, me * rows, rows, 0)
        tn = lambda a, b: lax.dot_general(a, b, (((0,), (0,)), ((), ())), preferred_element_type=F32)
        gw_o = jnp.dot(o_t, gy_all, preferred_element_type=F32).reshape(w_o.shape)
        gw_q = jnp.transpose(jnp.dot(dq_t, x_all, preferred_element_type=F32).reshape(heads, qk, width), (2, 0, 1))
        gw_uk = tn(latent, dk).reshape(w_uk.shape)
        gw_uv = tn(latent, dv).reshape(w_uv.shape)
        d_latent = mm(dk, wuk_cols, NT) + mm(dv, wuv_cols, NT)
        gg_kv = jnp.sum(d_latent * c_norm, axis=0)
        d_norm = d_latent * g_f32
        dc_raw = (inv_rms * (d_norm - c_norm * jnp.mean(d_norm * c_norm, axis=-1, keepdims=True))).astype(BF16)
        d_kr = (dkr[0] + dkr[1])[:, :rope_dim]
        r1, r2 = d_kr[:, :half], d_kr[:, half:]
        cos, sin = tab[:, :half], tab[:, LANES - half:]
        dkr_raw = jnp.concatenate([r1 * cos + r2 * sin, r2 * cos - r1 * sin], axis=1).astype(BF16)
        gw_dkv = tn(x_all, dc_raw)
        gw_kr = tn(dkr_raw, x_all).T
        dx_loc = dx_q + mm(own(dc_raw), w_dkv, NT) + mm(own(dkr_raw), w_kr, NT)
        return (y_loc, dx_loc.astype(BF16), gw_q, gw_dkv, gg_kv, gw_kr, gw_uk, gw_uv, gw_o)

    return jax.shard_map(device_fn, mesh=mesh, in_specs=in_specs, out_specs=out_specs, check_vma=False)
```

time: 1230 us -> 171 us (0.14)
  waiting for transfers between devices: 982 us -> 0 us
  Pallas kernels: 0 us -> 106 us
  matrix products: 105 us -> 47 us
  local copies, waits for them, and re-layouts: 64.5 us -> 10.1 us
  blocking collectives: 52 us -> 0 us
  between operations: 14.6 us -> 0.81 us
    psum x1 -> x0, waiting for transfers between devices: 536 us -> none  [device_fn(): lax.psum((gw_q, gw_dkv, gg_kv, gw_kr, gw_uk, gw_uv, gw_o), 'cp')]
    unnamed x7 -> x0, waiting for transfers between devices: 273 us -> none
    reduce_scatter x2 -> x0, waiting for transfers between devices: 127 us -> none  [the longest x1 65.2 us: device_fn(): lax.psum_scatter(dv_all, 'cp', scatter_dimension=0, tiled=True)]
    pallas_call x0 -> x1, Pallas kernels: none -> 106 us  [block(): pl.pallas_call(functools.partial(block_kernel, n_chips, qk, scale), out_s...]
    dot_general x40 -> x10, matrix products: 105 us -> 47 us  [the longest x1 16.7 us: device_fn(): jnp.dot(dq_t, x_all, preferred_element_type=F32).reshape(heads, qk, width)]
    all_gather x2 -> x0, waiting for transfers between devices: 46.2 us -> none  [the longest x1 39.8 us: device_fn(): k_nope_all = lax.all_gather(k_nope, 'cp', axis=0, tiled=True)]
    unnamed x76 -> x35, local copies, waits for them, and re-layouts: 47.5 us -> 10.1 us
    psum x1 -> x0, blocking collectives: 27.6 us -> none  [device_fn(): lax.psum((gw_q, gw_dkv, gg_kv, gw_kr, gw_uk, gw_uv, gw_o), 'cp')]
  transfers between devices with their start and end apart: 6 -> 0, of which waited for: 6 -> 0; matrix products, arithmetic and copies ran while one was open for 5% -> 0% of each run, Pallas kernels for 0% -> 0%
where the time goes in v1:
time: 171 us; the launch traced here: 170 us
  Pallas kernels  106 us (62%)
  matrix products  47 us (27%)
  local copies, waits for them, and re-layouts  10.1 us (6%)
  other arithmetic  6.52 us (4%)
    pallas_call x1, Pallas kernels, block(): pl.pallas_call(functools.partial(block_kernel, n_chips, qk, scale), out_s...  106 us
    dot_general x1, matrix products, device_fn(): jnp.dot(dq_t, x_all, preferred_element_type=F32).reshape(heads, qk, width)  16.7 us
    dot_general x1, matrix products, device_fn(): gw_o = jnp.dot(o_t, gy_all, preferred_element_type=F32).reshape(w_o.shape)  11.8 us
    dot_general x4, matrix products, device_fn(): lax.dot_general(a, b, (((0,), (0,)), ((), ())), preferred_element_type=F32)  11.1 us
    unnamed x35, local copies, waits for them, and re-layouts  10.1 us
    dot_general x4, matrix products, mm(): return lax.dot_general(lhs, rhs, dims, preferred_element_type=F32)  7.44 us

profile of v1, /device:TPU:21, one launch (start us, length us, event | category | flops | bytes accessed | tf_op | source)
XLA Modules:
  0.0 170.3 jit_solution(1824952042648377455)
XLA Ops:
  0.6 1.3 convert_element_type.10
  1.9 105.9 %latent_block.1 = (bf16[1024,2048]{1,0:T(8,128)(2,1)}, bf16[1024,2048]{1,0:T(8,128)(2,1)}, bf16[1024,512]{1,0:T(8,128)(2,1)}, f32[1024,512]{1,0:T(8,128)}, bf16[...) custom-call(bf16[64,2048]{1,0:T(8,128)(2,1)} %x_ref.1, ...), custom_call_target="tpu_custom_call" | custom-call | tf_op jit(solution)/shard_map/latent_block/pallas_call | solution.py:386
  107.8 0.0 copy-start.5
  107.8 2.0 %multiply_reduce_fusion.2 = f32[1024]{0:T(1024)S(1)} fusion(f32[1024,512]{1,0:T(8,128)} %get-tuple-element.22), kind=kLoop, calls=%fused_computation.14 | loop fusion | flops 1047552 | bytes 2101248 | tf_op jit(solution)/shard_map/reduce_sum | solution.py:424
  109.8 1.3 add_bitcast_fusion
  111.0 0.0 copy-start.1
  111.0 0.0 copy-start.6
  111.0 1.6 subtract_convert_fusion
  112.6 0.0 copy-done.5
  112.7 1.8 %fusion.10 = f32[2048,64]{0,1:T(8,128)} fusion(bf16[1024,2048]{1,0:T(8,128)(2,1)S(1)} %copy-done.5, bf16[1024,32]{1,0:T(8,128)(2,1)S(1)} %get-tuple-element.33, bf16[1024,32]{1,0:T(8,128)(2,1)S(1)} %get-tuple-element.34), kind=kOutput, calls=%fused_computation.19 | convolution fusion | flops 268697600 | bytes 4849664 | tf_op jit(solution)/shard_map/dot_general | solution.py:428
  114.4 0.0 copy-done.1
  114.4 0.0 copy-done.6
  114.4 0.0 copy-start.2
  114.4 2.4 %fusion.1 = f32[1024,512]{1,0:T(8,128)S(1)} fusion(bf16[1024,2048]{1,0:T(8,128)(2,1)S(1)} %copy-done.1, bf16[64,8,16,128]{3,2,1,0:T(8,128)(2,1)S(1)} %bitcast.49), kind=kOutput, calls=%fused_computation.5 | convolution fusion | flops 2147483648 | bytes 8388608 | tf_op jit(solution)/shard_map/dot_general | solution.py:24
  116.8 0.0 copy-done.2
  116.8 0.0 copy-start.11
  116.8 2.4 %convolution_bitcast_fusion = f32[64,8,16,128]{3,1,2,0:T(8,128)S(1)} fusion(bf16[1024,512]{1,0:T(8,128)(2,1)S(1)} %copy-done.2, bf16[1024,2048]{1,0:T(8,128)(2,1)S(1)} %copy-done.1), kind=kOutput, calls=%fused_computation.3 | convolution fusion | flops 2147483648 | bytes 9437184 | tf_op jit(solution)/shard_map/dot_general | solution.py:428
  119.3 0.0 copy-start
  119.3 0.0 copy-start.4
  119.3 0.0 copy-start.7
  119.3 3.1 %copy.24 = f32[64,8,16,128]{3,2,1,0:T(8,128)} copy(f32[64,8,16,128]{3,1,2,0:T(8,128)S(1)} %convolution_bitcast_fusion) | data formatting | bytes 8388608
  122.4 0.0 copy-done.11
  122.4 0.0 copy-done
  122.4 1.3 copy-done.4
  123.7 0.6 copy-done.7
  124.3 3.3 %multiply_reduce_fusion = (f32[512]{0:T(512)}, f32[1024]{0:T(1024)S(1)}, f32[1024,512]{1,0:T(8,128)S(1)}) fusion(f32[1024,512]{1,0:T(8,128)S(1)} %copy-done.4, f32[1024]{0:T(1024)S(1)} %add_rsqrt_fusion, f32[512]{0:T(512)S(1)} %copy-done.11, f32[1024,512]{1,0:T(8,128)S(1)} %fusion.1, bf16[1024,2048]{1,0:T(8,128)(2,1)S(1)} %copy-done, ...), kind=kOutput, calls=%fused_computation.11 | convolution fusion | flops 2151152128 | bytes 12595200 | tf_op jit(solution)/shard_map/dot_general | solution.py:24
  127.6 2.4 %convolution_bitcast_fusion.1 = f32[64,8,16,128]{3,1,2,0:T(8,128)S(1)} fusion(bf16[1024,512]{1,0:T(8,128)(2,1)S(1)} %copy-done.2, bf16[1024,2048]{1,0:T(8,128)(2,1)S(1)} %copy-done), kind=kOutput, calls=%fused_computation.4 | convolution fusion | flops 2147483648 | bytes 9437184 | tf_op jit(solution)/shard_map/dot_general | solution.py:428
  130.0 3.2 %copy.23 = f32[64,8,16,128]{3,2,1,0:T(8,128)} copy(f32[64,8,16,128]{3,1,2,0:T(8,128)S(1)} %convolution_bitcast_fusion.1) | data formatting | bytes 8388608
  133.2 0.0 copy-start.3
  133.2 0.0 copy-start.9
  133.2 0.0 copy-start.8
  133.2 0.4 multiply_convert_fusion
  133.7 1.1 copy-done.3
  134.8 0.1 copy-done.9
  134.9 0.8 convolution_add_fusion.1
  135.6 0.0 copy-done.8
  135.6 0.0 slice-start
  135.7 1.0 fusion
  136.6 4.5 %fusion.22 = f32[2048,512]{1,0:T(8,128)} fusion(bf16[1024,2048]{1,0:T(8,128)(2,1)S(1)} %copy-done.5, bf16[1024,512]{1,0:T(8,128)(2,1)S(1)} %multiply_convert_fusion), kind=kOutput, calls=%fused_computation.34 | convolution fusion | flops 2147483648 | bytes 9437184 | tf_op jit(solution)/shard_map/dot_general | solution.py:428
  141.1 0.0 slice-done
  141.1 0.0 slice-done.1
  141.1 0.0 copy-start.13
  141.1 16.7 %fusion.21 = f32[3072,2048]{1,0:T(8,128)} fusion(bf16[3072,1024]{1,0:T(8,128)(2,1)S(1)} %bitcast.54, bf16[1024,2048]{1,0:T(8,128)(2,1)S(1)} %copy-done.5), kind=kOutput, calls=%fused_computation.33 | convolution fusion | flops 12884901888 | bytes 35651584 | tf_op jit(solution)/shard_map/dot_general | solution.py:430
  157.8 0.0 copy-done.12
  157.8 0.0 copy-done.13
  157.8 11.8 %fusion.23 = f32[2048,2048]{1,0:T(8,128)} fusion(bf16[2048,1024]{1,0:T(8,128)(2,1)S(1)} %copy-done.13, bf16[1024,2048]{1,0:T(8,128)(2,1)S(1)} %copy-done.12), kind=kOutput, calls=%fused_computation.35 | convolution fusion | flops 8589934592 | bytes 25165824 | tf_op jit(solution)/shard_map/dot_general | solution.py:429
  169.6 0.0 copy-done.10
  169.6 0.7 copy.38
  (6 shorter events, 0.0 us)
Async XLA Ops:
  107.8 4.9 %copy-start.5 = (bf16[1024,2048]{1,0:T(8,128)(2,1)S(1)}, bf16[1024,2048]{1,0:T(8,128)(2,1)}, u32[]{:S(2)}) copy-start(bf16[1024,2048]{1,0:T(8,128)(2,1)} %get-tuple-element.27) | copy-start | bytes 12582916
  111.0 3.4 %copy-start.1 = (bf16[1024,2048]{1,0:T(8,128)(2,1)S(1)}, bf16[1024,2048]{1,0:T(8,128)(2,1)}, u32[]{:S(2)}) copy-start(bf16[1024,2048]{1,0:T(8,128)(2,1)} %get-tuple-element.24) | copy-start | bytes 12582916
  111.0 3.4 %copy-start.6 = (bf16[512,16,128]{2,1,0:T(8,128)(2,1)S(1)}, bf16[512,16,128]{2,1,0:T(8,128)(2,1)}, u32[]{:S(2)}) copy-start(bf16[512,16,128]{2,1,0:T(8,128)(2,1)} %wuv_ref.1) | copy-start | bytes 6291460
  114.4 2.4 %copy-start.2 = (bf16[1024,512]{1,0:T(8,128)(2,1)S(1)}, bf16[1024,512]{1,0:T(8,128)(2,1)}, u32[]{:S(2)}) copy-start(bf16[1024,512]{1,0:T(8,128)(2,1)} %get-tuple-element.28) | copy-start | bytes 3145732
  116.8 5.5 %copy-start.11 = (f32[512]{0:T(512)S(1)}, f32[512]{0:T(512)}, u32[]{:S(2)}) copy-start(f32[512]{0:T(512)} %convert_element_type.10) | copy-start | bytes 6148
  119.3 3.1 %copy-start = (bf16[1024,2048]{1,0:T(8,128)(2,1)S(1)}, bf16[1024,2048]{1,0:T(8,128)(2,1)}, u32[]{:S(2)}) copy-start(bf16[1024,2048]{1,0:T(8,128)(2,1)} %get-tuple-element.23) | copy-start | bytes 12582916
  119.3 4.4 %copy-start.4 = (f32[1024,512]{1,0:T(8,128)S(1)}, f32[1024,512]{1,0:T(8,128)}, u32[]{:S(2)}) copy-start(f32[1024,512]{1,0:T(8,128)} %get-tuple-element.22) | copy-start | bytes 6291460
  119.3 5.0 %copy-start.7 = (bf16[512,16,128]{2,1,0:T(8,128)(2,1)S(1)}, bf16[512,16,128]{2,1,0:T(8,128)(2,1)}, u32[]{:S(2)}) copy-start(bf16[512,16,128]{2,1,0:T(8,128)(2,1)} %wuk_ref.1) | copy-start | bytes 6291460
  133.2 1.6 copy-start.3
  133.2 1.7 copy-start.9
  133.2 2.4 %copy-start.8 = (bf16[2048,64]{0,1:T(8,128)(2,1)S(1)}, bf16[2048,64]{0,1:T(8,128)(2,1)}, u32[]{:S(2)}) copy-start(bf16[2048,64]{0,1:T(8,128)(2,1)} %param.15) | copy-start | bytes 786436
  135.6 5.5 %slice-start = ((s8[6291456]{0:T(1024)(128)(4,1)}), s8[4194304]{0:T(1024)(128)(4,1)S(1)}, s32[]{:S(2)}) async-start(s8[6291456]{0:T(1024)(128)(4,1)} %bitcast.53), calls=%async_computation | async-start | bytes 8388608
  136.6 4.5 %slice-start.1 = ((s8[6291456]{0:T(1024)(128)(4,1)}), s8[2097152]{0:T(1024)(128)(4,1)S(1)}, s32[]{:S(2)}) async-start(s8[6291456]{0:T(1024)(128)(4,1)} %bitcast.53), calls=%async_computation.1 | async-start | bytes 4194304
  141.1 16.7 %copy-start.12 = (bf16[1024,2048]{1,0:T(8,128)(2,1)S(1)}, bf16[1024,2048]{1,0:T(8,128)(2,1)}, u32[]{:S(2)}) copy-start(bf16[1024,2048]{1,0:T(8,128)(2,1)} %get-tuple-element.30) | copy-start | bytes 12582916
  141.1 16.7 %copy-start.13 = (bf16[2048,1024]{1,0:T(8,128)(2,1)S(1)}, bf16[2048,1024]{1,0:T(8,128)(2,1)}, u32[]{:S(2)}) copy-start(bf16[2048,1024]{1,0:T(8,128)(2,1)} %get-tuple-element.29) | copy-start | bytes 12582916
  157.8 11.8 %copy-start.10 = (bf16[64,2048]{1,0:T(8,128)(2,1)S(1)}, bf16[64,2048]{1,0:T(8,128)(2,1)}, u32[]{:S(2)}) copy-start(bf16[64,2048]{1,0:T(8,128)(2,1)} %get-tuple-element.45) | copy-start | bytes 786436

commit v2 on v1

--- a/solution.py
+++ b/solution.py
@@ -13,6 +13,7 @@
 QBLK = 256
 MASKED = -1e30
 LANES = 128
+PARTS = 4
 F32 = jnp.float32
 BF16 = jnp.bfloat16
 NN = (((1,), (0,)), ((), ()))
@@ -40,7 +41,7 @@
     partner = me + 1 - 2 * core
     ring_dev = (lax.rem(chip + 1, n_chips) * 2 + core, lax.rem(chip + n_chips - 1, n_chips) * 2 + core)
     rows = x_ref.shape[0]
-    part = rows // 2
+    part = rows // PARTS
     both = 2 * rows
     seq = x_s.shape[0]
     heads = wq_s.shape[0]
@@ -71,10 +72,7 @@
 
     def hop(arr, h, p):
         for d in range(2):
-            if isinstance(p, int):
-                limit = far if d == p else far - 1
-            else:
-                limit = jnp.where(p == d, far, far - 1)
+            limit = jnp.where(lax.div(p, PARTS // 2) == d, far, far - 1)
 
             @pl.when(h <= limit)
             def _():
@@ -112,11 +110,11 @@
     wo_copy(0).start()
     wo_copy(1).start()
     pl.semaphore_wait(barrier, 3)
-    for p in range(2):
+    for p in range(PARTS):
         for d in range(2):
             ring(0, d, 0, p, True).start()
     for arr in range(2):
-        for p in range(2):
+        for p in range(PARTS):
             across(arr, 0, p, True).start()
 
     wq_s[:, qk:, :] = jnp.zeros((heads, 2 * LANES - qk, wq_s.shape[2]), BF16)
@@ -133,43 +131,7 @@
         for hh in range(heads):
             wkv_s[hh, :, idx * nope:(idx + 1) * nope] = wkv_f32[pl.ds(hh, rank, stride=heads), :].astype(BF16)
 
-    lane = lax.broadcasted_iota(jnp.int32, (both, LANES), 1)
-
-    def project(stage, starts):
-        x_blk = jnp.concatenate([x_s[pl.ds(st, both), :] for st in starts], axis=0)
-        cos_l, sin_l = [], []
-        for st in starts:
-            tab = tab_s[pl.ds(st, both), :]
-            cos_l.append(jnp.where(lane < rope_dim, tab, 0.0))
-            sin_l.append(jnp.where(lane < rope_dim, pltpu.roll(tab, rope_dim, 1), 0.0))
-        cos_v, sin_v = jnp.concatenate(cos_l, axis=0), jnp.concatenate(sin_l, axis=0)
-
-        def rotate(t):
-            return (t * cos_v + swap_halves(t, half) * sin_v).astype(BF16)
-
-        def put(ref, val):
-            for idx, st in enumerate(starts):
-                ref[pl.ds(st, both), :] = val[idx * both:(idx + 1) * both, :]
-
-        if stage == 0:
-            c_raw = mm(x_blk, wdkv_s[...])
-            put(c_s, c_raw)
-            inv_rms = lax.rsqrt(jnp.mean(c_raw * c_raw, axis=-1, keepdims=True) + NORM_EPS)
-            put(lat_s, (c_raw * inv_rms * gkv_ref[...]).astype(BF16))
-            put(kr_s, rotate(mm(x_blk, wkr_s[...], NT)))
-
-        def head_pair(j, carry):
-            for hh in range(2):
-                h = stage * (heads // 2) + 2 * j + hh
-                q_raw = mm(x_blk, wq_s[h], NT)
-                q_val = jnp.concatenate([q_raw[:, :nope].astype(BF16), rotate(q_raw[:, nope:])], axis=1)
-                for idx, st in enumerate(starts):
-                    q_s[h, pl.ds(st, both), :] = q_val[idx * both:(idx + 1) * both, :]
-            return carry
-        lax.fori_loop(0, heads // 4, head_pair, 0)
-
-    hop(0, 1, 0)
-    hop(0, 1, 1)
+    lane = lax.broadcasted_iota(jnp.int32, (2 * both, LANES), 1)
 
     def x_stage(h, carry):
         near = h - 1
@@ -178,33 +140,60 @@
         chips = (lax.rem(chip + n_chips - up_rel, n_chips), lax.rem(chip + n_chips - dn_rel, n_chips))
         starts = [pl.multiple_of(c * both, both) for c in chips]
 
-        @pl.when(h <= far)
-        def _():
-            hop(0, h, 0)
-
-        @pl.when(h > far)
-        def _():
-            hop(1, 1, 0)
-        for p in range(2):
-            across(0, up_rel, p).wait_recv()
-            across(0, dn_rel, p).wait_recv()
-        project(0, starts)
-
-        @pl.when(h <= far)
-        def _():
-            hop(0, h, 1)
-
-        @pl.when(h == far - 1)
-        def _():
-            for p in range(2):
-                for d in range(2):
-                    ring(1, d, 0, p, True).start()
-
-        @pl.when(h > far)
-        def _():
-            hop(1, 1, 1)
-        project(1, starts)
+        def rows_of(ref):
+            return jnp.concatenate([ref[pl.ds(st, both), :] for st in starts], axis=0)
+
+        def put(ref, val):
+            for idx, st in enumerate(starts):
+                ref[pl.ds(st, both), :] = val[idx * both:(idx + 1) * both, :]
+
+        def rotate(t):
+            tab = rows_of(tab_s)
+            cos_v = jnp.where(lane < rope_dim, tab, 0.0)
+            sin_v = jnp.where(lane < rope_dim, pltpu.roll(tab, rope_dim, 1), 0.0)
+            return (t * cos_v + swap_halves(t, half) * sin_v).astype(BF16)
+
+        def quarter(j, carry):
+            @pl.when(h <= far)
+            def _():
+                hop(0, h, j)
+
+            @pl.when(h > far)
+            def _():
+                hop(1, 1, j)
+
+            @pl.when((h == far - 1) & (j == PARTS - 1))
+            def _():
+                for p in range(PARTS):
+                    for d in range(2):
+                        ring(1, d, 0, p, True).start()
+
+            @pl.when(j == 0)
+            def _():
+                for p in range(PARTS):
+                    across(0, up_rel, p).wait_recv()
+                    across(0, dn_rel, p).wait_recv()
+                x_blk = rows_of(x_s)
+                c_raw = mm(x_blk, wdkv_s[...])
+                put(c_s, c_raw)
+                inv_rms = lax.rsqrt(jnp.mean(c_raw * c_raw, axis=-1, keepdims=True) + NORM_EPS)
+                put(lat_s, (c_raw * inv_rms * gkv_ref[...]).astype(BF16))
+                put(kr_s, rotate(mm(x_blk, wkr_s[...], NT)))
+            x_blk = rows_of(x_s)
+            for hh in range(heads // PARTS):
+                head = j * (heads // PARTS) + hh
+                q_raw = mm(x_blk, wq_s[head], NT)
+                q_val = jnp.concatenate([q_raw[:, :nope].astype(BF16), rotate(q_raw[:, nope:])], axis=1)
+                for idx, st in enumerate(starts):
+                    q_s[head, pl.ds(st, both), :] = q_val[idx * both:(idx + 1) * both, :]
+            return carry
+        lax.fori_loop(0, PARTS, quarter, 0)
         return carry
+
+    def first_hop(p, carry):
+        hop(0, 1, p)
+        return carry
+    lax.fori_loop(0, PARTS, first_hop, 0)
     lax.fori_loop(2, far + 2, x_stage, 0)
 
     outs = [pltpu.make_async_copy(src, dst, out_sem.at[idx]) for idx, (src, dst) in enumerate(((x_s, x_out), (lat_s, lat_out), (c_s, c_out), (gy_s, gy_out)))]
@@ -225,9 +214,12 @@
         return diag if i == 0 else jnp.concatenate([st[:i * QBLK, :], diag], axis=0)
 
     def forward(h, carry):
-        @pl.when(h < 2 * (far - 1))
-        def _():
-            hop(1, 2 + lax.div(h, 2), lax.rem(h, 2))
+        point = jnp.where(h < heads // 2, 2 * h, h + heads // 2)
+        hop(1, 2 + lax.div(point, PARTS), lax.rem(point, PARTS))
+
+        @pl.when(h < heads // 2)
+        def _():
+            hop(1, 2 + lax.div(point + 1, PARTS), lax.rem(point + 1, PARTS))
         kv = mm(lat_s[...], wkv_s[h]).astype(BF16)
         kn_s[h] = kv[:, :nope]
         v_s[h] = kv[:, nope:]
@@ -251,7 +243,7 @@
     ot_local.start()
     ot_remote.start()
     for rel in range(n_chips):
-        for p in range(2):
+        for p in range(PARTS):
             across(1, rel, p).wait_recv()
     outs[3].start()
 
@@ -332,9 +324,9 @@
     for copy in sums + [kr_local, kr_remote]:
         copy.start()
     for arr in range(2):
-        for p in range(2):
+        for p in range(PARTS):
             for d in range(2):
-                for h in range(far if d == p else far - 1):
+                for h in range(far if d == p // (PARTS // 2) else far - 1):
                     ring(arr, d, h, p, h == 0).wait_send()
             for rel in range(n_chips):
                 across(arr, rel, p, rel == 0).wait_send()
@@ -382,7 +374,7 @@
                vm((seq, 2 * nope), BF16), vm((2 * nope, seq), BF16), vm((seq, 2 * LANES), F32), vm((seq, nope), F32), vm((seq, LANES), F32),
                vm((2 * rows, width), F32), vm((2 * rows, width), F32), vm((rows, width), F32), vm((rows, width), F32),
                vm((2, 2 * qk, seq), BF16), vm((2, seq, 2 * nope), BF16), vm((2, seq, 2 * nope), BF16),
-               dma((2, 2, far, 2)), dma((2, 2, far, 2)), dma((2, n_chips, 2)), dma((2, n_chips, 2)), dma((7,)), dma((heads,)), dma((2,)), dma((4,)), dma((2, 3)), dma((2, 3)), dma((n_pairs, 3)), dma((6,)), dma((4,))]
+               dma((2, 2, far, PARTS)), dma((2, 2, far, PARTS)), dma((2, n_chips, PARTS)), dma((2, n_chips, PARTS)), dma((7,)), dma((heads,)), dma((2,)), dma((4,)), dma((2, 3)), dma((2, 3)), dma((n_pairs, 3)), dma((6,)), dma((4,))]
     return pl.pallas_call(
         functools.partial(block_kernel, n_chips, qk, scale),
         out_shape=(sds((seq, width), BF16), sds((seq, width), BF16), sds((seq, rank), BF16), sds((seq, rank), F32), sds((n_hv, seq), BF16), sds((n_feat, seq), BF16), sds((seq, n_hv), BF16), sds((seq, n_hv), BF16), sds((2, seq, LANES), F32), sds((rows, width), BF16), sds((rows, width), F32)),
@@ -392,6 +384,108 @@
         compiler_params=pltpu.CompilerParams(collective_id=0, has_side_effects=True, vmem_limit_bytes=67043328),
         name='latent_block',
     )(x_loc, gy_loc, tab, wq_rows, w_dkv, g_row, wkr_t, w_uk, w_uv, wo_rows)
+
+
+def grads_kernel(tile, ot_ref, dqt_ref, gy_ref, x_ref, lat_ref, dk_ref, dv_ref, gwo_ref, gwq_ref, guk_ref, guv_ref,
+                 lhs_s, rhs_s, lat_s, latt_s, kv_s, stage, stage_kv, in_sem, out_sem, kv_sem):
+    n_o, n_q = ot_ref.shape[0] // tile, dqt_ref.shape[0] // tile
+    heads = kv_s.shape[2] // LANES
+    rank = lat_s.shape[1]
+    n_c = rank // tile
+    rest = [(ot_ref.at[pl.ds(tile, (n_o - 1) * tile), :], lhs_s.at[pl.ds(tile, (n_o - 1) * tile), :]), (x_ref, rhs_s.at[1]), (dqt_ref, lhs_s.at[pl.ds(n_o * tile, n_q * tile), :]), (lat_ref, lat_s), (dk_ref, kv_s.at[0]), (dv_ref, kv_s.at[1])]
+    loads = [pltpu.make_async_copy(src, dst, in_sem.at[idx]) for idx, (src, dst) in enumerate([(ot_ref.at[pl.ds(0, tile), :], lhs_s.at[pl.ds(0, tile), :]), (gy_ref, rhs_s.at[0])] + rest)]
+    for copy in loads:
+        copy.start()
+
+    def out_copy(t, dst, base):
+        slot = lax.rem(t, 2)
+        return pltpu.make_async_copy(stage.at[slot], dst.at[pl.ds(pl.multiple_of((t - base) * tile, tile), tile), :], out_sem.at[slot])
+
+    loads[0].wait()
+    loads[1].wait()
+
+    def product(t, carry):
+        slot = lax.rem(t, 2)
+
+        @pl.when(t == 1)
+        def _():
+            loads[2].wait()
+
+        @pl.when(t == n_o)
+        def _():
+            loads[3].wait()
+            loads[4].wait()
+
+        @pl.when(t >= 2)
+        def _():
+            out_copy(t, gwo_ref, t).wait()
+        which = jnp.where(t < n_o, 0, 1)
+        stage[slot] = mm(lhs_s[pl.ds(pl.multiple_of(t * tile, tile), tile), :], rhs_s[which])
+
+        @pl.when(t < n_o)
+        def _():
+            out_copy(t, gwo_ref, 0).start()
+
+        @pl.when(t >= n_o)
+        def _():
+            out_copy(t, gwq_ref, n_o).start()
+        return carry
+    lax.fori_loop(0, n_o + n_q, product, 0)
+    for copy in loads[5:]:
+        copy.wait()
+    latt_s[...] = lat_s[...].T
+
+    def kv_copy(t, dst, base):
+        slot = lax.rem(t, 2)
+        size = tile * heads
+        return pltpu.make_async_copy(stage_kv.at[slot], dst.at[pl.ds(pl.multiple_of((t - base) * size, size), size), :], kv_sem.at[slot])
+
+    def latent_side(t, carry):
+        slot = lax.rem(t, 2)
+
+        @pl.when(t >= 2)
+        def _():
+            kv_copy(t, guk_ref, t).wait()
+        which = jnp.where(t < n_c, 0, 1)
+        row = pl.multiple_of((t - which * n_c) * tile, tile)
+        res = mm(latt_s[pl.ds(row, tile), :], kv_s[which])
+        for h in range(heads):
+            stage_kv[slot, pl.ds(h, tile, stride=heads), :] = res[:, h * LANES:(h + 1) * LANES]
+
+        @pl.when(t < n_c)
+        def _():
+            kv_copy(t, guk_ref, 0).start()
+
+        @pl.when(t >= n_c)
+        def _():
+            kv_copy(t, guv_ref, n_c).start()
+        return carry
+    lax.fori_loop(0, 2 * n_c, latent_side, 0)
+    for t in range(2):
+        out_copy(t, gwo_ref, t).wait()
+        kv_copy(t, guk_ref, t).wait()
+
+
+def big_grads(o_t, dq_t, gy_all, x_all, latent, dk, dv):
+    tile = 256
+    seq, width = x_all.shape
+    n_hv, n_feat, rank = o_t.shape[0], dq_t.shape[0], latent.shape[1]
+    heads = n_hv // LANES
+    hbm = pl.BlockSpec(memory_space=pl.ANY)
+    dma = pltpu.SemaphoreType.DMA
+    vm = pltpu.VMEM
+    sds = jax.ShapeDtypeStruct
+    flops = 2 * seq * width * (n_hv + n_feat) + 4 * seq * rank * n_hv
+    return pl.pallas_call(
+        functools.partial(grads_kernel, tile),
+        out_shape=(sds((n_hv, width), F32), sds((n_feat, width), F32), sds((rank * heads, LANES), F32), sds((rank * heads, LANES), F32)),
+        in_specs=[hbm] * 7,
+        out_specs=[hbm] * 4,
+        scratch_shapes=[vm((n_hv + n_feat, seq), BF16), vm((2, seq, width), BF16), vm((seq, rank), BF16), vm((rank, seq), BF16), vm((2, seq, n_hv), BF16), vm((2, tile, width), F32), vm((2, tile * heads, LANES), F32), dma((8,)), dma((2,)), dma((2,))],
+        compiler_params=pltpu.CompilerParams(vmem_limit_bytes=56 * 1024 * 1024),
+        cost_estimate=pl.CostEstimate(flops=flops, bytes_accessed=80 * 1024 * 1024, transcendentals=0),
+        name='weight_grads',
+    )(o_t, dq_t, gy_all, x_all, latent, dk, dv)
 
 
 def solution(mesh):
@@ -426,10 +520,10 @@
 
         own = lambda t: lax.dynamic_slice_in_dim(t, me * rows, rows, 0)
         tn = lambda a, b: lax.dot_general(a, b, (((0,), (0,)), ((), ())), preferred_element_type=F32)
-        gw_o = jnp.dot(o_t, gy_all, preferred_element_type=F32).reshape(w_o.shape)
-        gw_q = jnp.transpose(jnp.dot(dq_t, x_all, preferred_element_type=F32).reshape(heads, qk, width), (2, 0, 1))
-        gw_uk = tn(latent, dk).reshape(w_uk.shape)
-        gw_uv = tn(latent, dv).reshape(w_uv.shape)
+        gwo, gwq, guk, guv = big_grads(o_t, dq_t, gy_all, x_all, latent, dk, dv)
+        gw_o = gwo.reshape(w_o.shape)
+        gw_q = jnp.transpose(gwq.reshape(heads, qk, width), (2, 0, 1))
+        gw_uk, gw_uv = guk.reshape(w_uk.shape), guv.reshape(w_uv.shape)
         d_latent = mm(dk, wuk_cols, NT) + mm(dv, wuv_cols, NT)
         gg_kv = jnp.sum(d_latent * c_norm, axis=0)
         d_norm = d_latent * g_f32

time: 171 us -> 167 us (0.977)
  Pallas kernels: 106 us -> 142 us
  matrix products: 47 us -> 17.1 us
  local copies, waits for them, and re-layouts: 10.1 us -> 2.72 us
  other arithmetic: 6.52 us -> 3.98 us
    pallas_call x0 -> x1, Pallas kernels: none -> 36.4 us  [big_grads(): pl.pallas_call(functools.partial(grads_kernel, tile), out_shape=(sds((n_h...]
    dot_general x2 -> x0, matrix products: 28.5 us -> none  [the longest x1 16.7 us: device_fn(): jnp.dot(dq_t, x_all, preferred_element_type=F32).reshape(heads, qk, width)]
    unnamed x35 -> x25, local copies, waits for them, and re-layouts: 10.1 us -> 2.72 us
    dot_general x4 -> x2, matrix products: 11.1 us -> 6.14 us  [device_fn(): lax.dot_general(a, b, (((0,), (0,)), ((), ())), preferred_element_type=F32)]
    dot_general x4, matrix products: 7.44 us -> 11 us  [mm(): return lax.dot_general(lhs, rhs, dims, preferred_element_type=F32)]
where the time goes in v2:
time: 167 us
  Pallas kernels  142 us (85%)
  matrix products  17.1 us (10%)
  other arithmetic  3.98 us (2%)
  local copies, waits for them, and re-layouts  2.72 us (2%)
    pallas_call x1, Pallas kernels, block(): pl.pallas_call(functools.partial(block_kernel, n_chips, qk, scale), out_s...  106 us
    pallas_call x1, Pallas kernels, big_grads(): pl.pallas_call(functools.partial(grads_kernel, tile), out_shape=(sds((n_h...  36.4 us
    dot_general x4, matrix products, mm(): return lax.dot_general(lhs, rhs, dims, preferred_element_type=F32)  11 us
    dot_general x2, matrix products, device_fn(): lax.dot_general(a, b, (((0,), (0,)), ((), ())), preferred_element_type=F32)  6.14 us

profile of v2, /device:TPU:21, one launch (start us, length us, event | category | flops | bytes accessed | tf_op | source)
XLA Modules:
  0.0 167.0 jit_solution(7232239932094513618)
XLA Ops:
  0.6 1.3 convert_element_type.10
  1.9 106.0 %latent_block.1 = (bf16[1024,2048]{1,0:T(8,128)(2,1)}, bf16[1024,2048]{1,0:T(8,128)(2,1)}, bf16[1024,512]{1,0:T(8,128)(2,1)}, f32[1024,512]{1,0:T(8,128)}, bf16[...) custom-call(bf16[64,2048]{1,0:T(8,128)(2,1)} %x_ref.1, ...), custom_call_target="tpu_custom_call" | custom-call | tf_op jit(solution)/shard_map/latent_block/pallas_call | solution.py:378
  107.9 0.0 copy-start.3
  107.9 2.0 %multiply_reduce_fusion.2 = f32[1024]{0:T(1024)S(1)} fusion(f32[1024,512]{1,0:T(8,128)} %get-tuple-element.26), kind=kLoop, calls=%fused_computation.12 | loop fusion | flops 1047552 | bytes 2101248 | tf_op jit(solution)/shard_map/reduce_sum | solution.py:518
  109.9 0.2 copy-done.3
  110.1 0.0 copy-start.1
  110.1 0.0 copy-start.4
  110.1 0.0 copy-start.10
  110.1 0.0 copy-start.11
  110.1 4.7 %fusion.1 = f32[1024,512]{1,0:T(8,128)S(1)} fusion(bf16[1024,2048]{1,0:T(8,128)(2,1)} %get-tuple-element.28.dv_ref, bf16[64,8,16,128]{3,2,1,0:T(8,128)(2,1)S(1)} %bitcast.35), kind=kOutput, calls=%fused_computation.3 | convolution fusion | flops 2147483648 | bytes 8388608 | tf_op jit(solution)/shard_map/dot_general | solution.py:25
  114.9 0.0 copy-done.1
  114.9 0.0 copy-done.4
  114.9 0.0 copy-done.10
  114.9 0.0 copy-done.11
  114.9 3.3 %multiply_reduce_fusion = (f32[512]{0:T(512)}, f32[1024]{0:T(1024)S(1)}, f32[1024,512]{1,0:T(8,128)S(1)}) fusion(f32[1024,512]{1,0:T(8,128)S(1)} %copy-done.1, f32[1024]{0:T(1024)S(1)} %add_rsqrt_fusion, f32[512]{0:T(512)S(1)} %copy-done.10, f32[1024,512]{1,0:T(8,128)S(1)} %fusion.1, bf16[1024,2048]{1,0:T(8,128)(2,1)S(1)} %copy-done.11, ...), kind=kOutput, calls=%fused_computation.9 | convolution fusion | flops 2151152128 | bytes 12595200 | tf_op jit(solution)/shard_map/dot_general | solution.py:25
  118.2 0.0 copy-start
  118.2 0.4 multiply_convert_fusion
  118.7 1.1 copy-done
  119.8 0.0 copy-start.6
  119.8 0.0 copy-start.7
  119.8 0.0 copy-start.8
  119.8 1.9 %convolution_add_fusion.1 = f32[64,2048]{1,0:T(8,128)S(1)} fusion(f32[64,2048]{1,0:T(8,128)} %get-tuple-element.25, bf16[2048,512]{1,0:T(8,128)(2,1)S(1)} %copy-done, bf16[1024,512]{1,0:T(8,128)(2,1)S(1)} %multiply_convert_fusion, s32[]{:T(128)S(6)} %select_n.4), kind=kOutput, calls=%fused_computation.1 | convolution fusion | flops 134348800 | bytes 3211268 | tf_op jit(solution)/shard_map/dot_general | solution.py:25
  121.8 0.0 copy-done.6
  121.8 0.0 copy-start.5
  121.8 0.1 add_bitcast_fusion
  121.8 0.0 copy-done.7
  121.9 0.0 copy-done.8
  121.9 0.3 subtract_convert_fusion
  122.1 0.6 copy-done.5
  122.7 1.0 fusion
  123.7 0.0 copy-start.2
  123.7 36.4 %weight_grads.1 = (f32[2048,2048]{1,0:T(8,128)}, f32[3072,2048]{1,0:T(8,128)}, f32[8192,128]{1,0:T(8,128)}, f32[8192,128]{1,0:T(8,128)}) custom-call(bf16[2048,1024]{1,0:T(8,128)(2,1)} %get-tuple-element.30.ot_ref, bf16[3072,1024]{1,0:T(8,128)(2,1)} %get-tuple-element.31.dqt_ref, bf16[1024,2048]{1,0:T(8,128)(2,1)} %get-tuple-element.32.gy_ref, ...), custom_call_target="tpu_custom_call" | custom-call | flops 25769803776 | bytes 83886080 | tf_op jit(solution)/shard_map/weight_grads/pallas_call | solution.py:479
  160.1 0.0 copy-done.2
  160.1 4.4 %fusion.21 = f32[2048,512]{1,0:T(8,128)} fusion(bf16[1024,2048]{1,0:T(8,128)(2,1)S(1)} %copy-done.2, bf16[1024,512]{1,0:T(8,128)(2,1)S(1)} %multiply_convert_fusion), kind=kOutput, calls=%fused_computation.31 | convolution fusion | flops 2147483648 | bytes 9437184 | tf_op jit(solution)/shard_map/dot_general | solution.py:522
  164.5 0.0 copy-start.9
  164.5 1.8 %fusion.10 = f32[2048,64]{0,1:T(8,128)} fusion(bf16[1024,2048]{1,0:T(8,128)(2,1)S(1)} %copy-done.2, bf16[1024,32]{1,0:T(8,128)(2,1)S(1)} %get-tuple-element.41, bf16[1024,32]{1,0:T(8,128)(2,1)S(1)} %get-tuple-element.42), kind=kOutput, calls=%fused_computation.17 | convolution fusion | flops 268697600 | bytes 4849664 | tf_op jit(solution)/shard_map/dot_general | solution.py:522
  166.3 0.0 copy-done.9
  166.3 0.7 copy.36
  (2 shorter events, 0.0 us)
Async XLA Ops:
  107.9 2.2 %copy-start.3 = (bf16[512,16,128]{2,1,0:T(8,128)(2,1)S(1)}, bf16[512,16,128]{2,1,0:T(8,128)(2,1)}, u32[]{:S(2)}) copy-start(bf16[512,16,128]{2,1,0:T(8,128)(2,1)} %wuv_ref.1) | copy-start | bytes 6291460
  110.1 4.7 %copy-start.1 = (f32[1024,512]{1,0:T(8,128)S(1)}, f32[1024,512]{1,0:T(8,128)}, u32[]{:S(2)}) copy-start(f32[1024,512]{1,0:T(8,128)} %get-tuple-element.26) | copy-start | bytes 6291460
  110.1 4.7 %copy-start.4 = (bf16[512,16,128]{2,1,0:T(8,128)(2,1)S(1)}, bf16[512,16,128]{2,1,0:T(8,128)(2,1)}, u32[]{:S(2)}) copy-start(bf16[512,16,128]{2,1,0:T(8,128)(2,1)} %wuk_ref.1) | copy-start | bytes 6291460
  110.1 4.8 %copy-start.10 = (f32[512]{0:T(512)S(1)}, f32[512]{0:T(512)}, u32[]{:S(2)}) copy-start(f32[512]{0:T(512)} %convert_element_type.10) | copy-start | bytes 6148
  110.1 4.8 %copy-start.11 = (bf16[1024,2048]{1,0:T(8,128)(2,1)S(1)}, bf16[1024,2048]{1,0:T(8,128)(2,1)}, u32[]{:S(2)}) copy-start(bf16[1024,2048]{1,0:T(8,128)(2,1)} %get-tuple-element.27.dk_ref) | copy-start | bytes 12582916
  118.2 1.6 copy-start
  119.8 1.9 %copy-start.6 = (f32[2,1024,128]{2,1,0:T(8,128)S(1)}, f32[2,1024,128]{2,1,0:T(8,128)}, u32[]{:S(2)}) copy-start(f32[2,1024,128]{2,1,0:T(8,128)} %get-tuple-element.29) | copy-start | bytes 3145732
  119.8 2.0 %copy-start.7 = (f32[1024,32]{1,0:T(8,128)S(1)}, f32[1024,32]{1,0:T(8,128)}, u32[]{:S(2)}) copy-start(f32[1024,32]{1,0:T(8,128)} %constant.22) | copy-start | bytes 393220
  119.8 2.0 %copy-start.8 = (f32[1024,32]{1,0:T(8,128)S(1)}, f32[1024,32]{1,0:T(8,128)}, u32[]{:S(2)}) copy-start(f32[1024,32]{1,0:T(8,128)} %constant.23) | copy-start | bytes 393220
  121.8 1.0 copy-start.5
  123.7 36.4 %copy-start.2 = (bf16[1024,2048]{1,0:T(8,128)(2,1)S(1)}, bf16[1024,2048]{1,0:T(8,128)(2,1)}, u32[]{:S(2)}) copy-start(bf16[1024,2048]{1,0:T(8,128)(2,1)} %get-tuple-element.33.x_ref) | copy-start | bytes 12582916
  164.5 1.8 %copy-start.9 = (bf16[64,2048]{1,0:T(8,128)(2,1)S(1)}, bf16[64,2048]{1,0:T(8,128)(2,1)}, u32[]{:S(2)}) copy-start(bf16[64,2048]{1,0:T(8,128)(2,1)} %get-tuple-element.53) | copy-start | bytes 786436

commit v3 on v2

--- a/solution.py
+++ b/solution.py
@@ -30,11 +30,11 @@
 
 
 def block_kernel(n_chips, qk, scale, x_ref, gy_ref, tab_ref, wq_ref, wdkv_ref, gkv_ref, wkr_ref, wuk_ref, wuv_ref, wo_ref,
-                 x_out, gy_out, lat_out, c_out, ot_out, dqt_out, dk_out, dv_out, dkr_out, y_out, dx_out,
+                 x_out, gy_out, lat_out, c_out, ot_out, dqt_out, dk_out, dv_out, dkr_out, dlat_out, y_out, dx_out,
                  x_s, gy_s, tab_s, tabt_s, wq_s, wdkv_s, wkr_s, wkv_raw, wkv_f32, wkv_s, wo_s, q_s, lat_s, c_s, kr_s, krt_s,
                  kn_s, v_s, kt_s, vt_s, lse_s, ot_st, do_s, dot_s, dk_acc, dv_acc, dkr_acc, y_acc, dx_acc, y_buf, dx_buf,
                  dqt_st, dk_st, dv_st,
-                 ring_send, ring_recv, pr_send, pr_recv, w_sem, wq_sem, wo_sem, out_sem, loc_sem, snd_sem, rcv_sem, kr_sem, yx_sem):
+                 ring_send, ring_recv, pr_send, pr_recv, w_sem, wq_sem, wo_sem, out_sem, loc_sem, snd_sem, rcv_sem, kr_sem, yx_sem, dlat_sem):
     me = lax.axis_index('cp')
     core = lax.rem(me, 2)
     chip = lax.div(me, 2)
@@ -85,11 +85,11 @@
 
     def weight_copies():
         first = core * heads
-        out = [pltpu.make_async_copy(wdkv_ref, wdkv_s, w_sem.at[0]),
+        out = [pltpu.make_async_copy(wuk_ref.at[:, pl.ds(pl.multiple_of(first, heads), heads), :], wkv_raw.at[0], w_sem.at[2]),
+               pltpu.make_async_copy(wuv_ref.at[:, pl.ds(pl.multiple_of(first, heads), heads), :], wkv_raw.at[1], w_sem.at[3]),
                pltpu.make_async_copy(wkr_ref, wkr_s.at[pl.ds(0, rope_dim), :], w_sem.at[1]),
-               pltpu.make_async_copy(wuk_ref.at[:, pl.ds(pl.multiple_of(first, heads), heads), :], wkv_raw.at[0], w_sem.at[2]),
-               pltpu.make_async_copy(wuv_ref.at[:, pl.ds(pl.multiple_of(first, heads), heads), :], wkv_raw.at[1], w_sem.at[3]),
-               pltpu.make_async_copy(tab_ref, tab_s, w_sem.at[4])]
+               pltpu.make_async_copy(tab_ref, tab_s, w_sem.at[4]),
+               pltpu.make_async_copy(wdkv_ref, wdkv_s, w_sem.at[0])]
         for idx in range(2):
             out.append(pltpu.make_async_copy(srcs[idx], bufs[idx].at[pl.ds(pl.multiple_of(me * rows, rows), rows), :], w_sem.at[5 + idx]))
         for hh in range(heads):
@@ -105,10 +105,6 @@
     barrier = pltpu.get_barrier_semaphore()
     for peer in (ring_dev[0], ring_dev[1], partner):
         pl.semaphore_signal(barrier, inc=1, device_id={'cp': peer}, device_id_type=mesh_id)
-    for copy in weight_copies():
-        copy.start()
-    wo_copy(0).start()
-    wo_copy(1).start()
     pl.semaphore_wait(barrier, 3)
     for p in range(PARTS):
         for d in range(2):
@@ -116,20 +112,30 @@
     for arr in range(2):
         for p in range(PARTS):
             across(arr, 0, p, True).start()
-
-    wq_s[:, qk:, :] = jnp.zeros((heads, 2 * LANES - qk, wq_s.shape[2]), BF16)
-    wkr_s[rope_dim:, :] = jnp.zeros((LANES - rope_dim, wkr_s.shape[1]), BF16)
-    dkr_acc[...] = jnp.zeros_like(dkr_acc)
-    y_acc[...] = jnp.zeros_like(y_acc)
-    dx_acc[...] = jnp.zeros_like(dx_acc)
     for copy in weight_copies():
+        copy.start()
+    wo_copy(0).start()
+    wo_copy(1).start()
+
+    weights = weight_copies()
+    rank = wkv_raw.shape[1]
+    for p in range(PARTS):
+        hop(0, 1, p)
+        if p == 0:
+            wq_s[:, qk:, :] = jnp.zeros((heads, 2 * LANES - qk, wq_s.shape[2]), BF16)
+            wkr_s[rope_dim:, :] = jnp.zeros((LANES - rope_dim, wkr_s.shape[1]), BF16)
+            dkr_acc[...] = jnp.zeros_like(dkr_acc)
+            y_acc[...] = jnp.zeros_like(y_acc)
+            dx_acc[...] = jnp.zeros_like(dx_acc)
+        elif p <= 2:
+            idx = p - 1
+            weights[idx].wait()
+            wkv_f32[...] = wkv_raw[idx].astype(F32).reshape(rank * heads, LANES)
+            for hh in range(heads):
+                wkv_s[hh, :, idx * nope:(idx + 1) * nope] = wkv_f32[pl.ds(hh, rank, stride=heads), :].astype(BF16)
+    for copy in weights[2:]:
         copy.wait()
     tabt_s[...] = tab_s[...].T
-    rank = wkv_raw.shape[1]
-    for idx in range(2):
-        wkv_f32[...] = wkv_raw[idx].astype(F32).reshape(rank * heads, LANES)
-        for hh in range(heads):
-            wkv_s[hh, :, idx * nope:(idx + 1) * nope] = wkv_f32[pl.ds(hh, rank, stride=heads), :].astype(BF16)
 
     lane = lax.broadcasted_iota(jnp.int32, (2 * both, LANES), 1)
 
@@ -190,10 +196,6 @@
         lax.fori_loop(0, PARTS, quarter, 0)
         return carry
 
-    def first_hop(p, carry):
-        hop(0, 1, p)
-        return carry
-    lax.fori_loop(0, PARTS, first_hop, 0)
     lax.fori_loop(2, far + 2, x_stage, 0)
 
     outs = [pltpu.make_async_copy(src, dst, out_sem.at[idx]) for idx, (src, dst) in enumerate(((x_s, x_out), (lat_s, lat_out), (c_s, c_out), (gy_s, gy_out)))]
@@ -246,18 +248,24 @@
         for p in range(PARTS):
             across(1, rel, p).wait_recv()
     outs[3].start()
-
-    def pair_copies(step):
+    outs[2].wait()
+    c_s[...] = jnp.zeros_like(c_s)
+
+    def head_copies(step, hh):
         slot_of = lax.rem(step, 2)
-        pair = core * n_pairs + step
-        col = pl.ds(pl.multiple_of(pair * 2 * nope, 2 * nope), 2 * nope)
-        regions = ((dqt_st.at[slot_of], dqt_out.at[pl.ds(pl.multiple_of(pair * 2 * qk, 2 * qk), 2 * qk), :]), (dk_st.at[slot_of], dk_out.at[:, col]), (dv_st.at[slot_of], dv_out.at[:, col]))
+        head = (core * n_pairs + step) * 2 + hh
+        col = pl.ds(pl.multiple_of(head * nope, nope), nope)
+        cols = pl.ds(hh * nope, nope)
+        regions = ((dqt_st.at[slot_of, pl.ds(hh * qk, qk), :], dqt_out.at[pl.ds(pl.multiple_of(head * qk, qk), qk), :]), (dk_st.at[slot_of, :, cols], dk_out.at[:, col]), (dv_st.at[slot_of, :, cols], dv_out.at[:, col]))
         local, remote = [], []
         for idx, (src, dst) in enumerate(regions):
-            local.append(pltpu.make_async_copy(src, dst, loc_sem.at[slot_of, idx]))
-            remote.append(pltpu.make_async_remote_copy(src_ref=src, dst_ref=dst, send_sem=snd_sem.at[slot_of, idx], recv_sem=rcv_sem.at[step, idx], device_id={'cp': partner}, device_id_type=mesh_id))
+            local.append(pltpu.make_async_copy(src, dst, loc_sem.at[slot_of, hh, idx]))
+            remote.append(pltpu.make_async_remote_copy(src_ref=src, dst_ref=dst, send_sem=snd_sem.at[slot_of, hh, idx], recv_sem=rcv_sem.at[step, hh, idx], device_id={'cp': partner}, device_id_type=mesh_id))
         return local, remote
 
+    theirs = pl.ds(pl.multiple_of((1 - core) * rows, rows), rows)
+    mine = pl.ds(pl.multiple_of(core * rows, rows), rows)
+    sums = [pltpu.make_async_remote_copy(src_ref=acc.at[theirs, :], dst_ref=buf, send_sem=yx_sem.at[idx], recv_sem=yx_sem.at[2 + idx], device_id={'cp': partner}, device_id_type=mesh_id) for idx, (acc, buf) in enumerate(((y_acc, y_buf), (dx_acc, dx_buf)))]
     chip_cols = pl.ds(pl.multiple_of(chip * both, both), both)
 
     def backward(g, carry):
@@ -265,15 +273,21 @@
 
         @pl.when(g >= 2)
         def _():
-            local, remote = pair_copies(g - 2)
-            for copy in local:
-                copy.wait()
-            for copy in remote:
-                copy.wait_send()
+            for hh in range(2):
+                local, remote = head_copies(g - 2, hh)
+                for copy in local:
+                    copy.wait()
+                for copy in remote:
+                    copy.wait_send()
         wo_copy(g).wait()
         do_all = mm(gy_s[...], wo_s[slot], NT).astype(BF16)
         do_s[...] = do_all
         dot_s[...] = do_all.T
+        y_acc[...] += mm(ot_st[pl.ds(pl.multiple_of(g * 2 * nope, 2 * nope), 2 * nope), chip_cols], wo_s[slot], TN)
+
+        @pl.when(g == n_pairs - 1)
+        def _():
+            sums[0].start()
         for hh in range(2):
             h = 2 * g + hh
             cols = slice(hh * nope, (hh + 1) * nope)
@@ -303,12 +317,13 @@
                 dqt_st[slot, hh * qk:(hh + 1) * qk, blk] = dqt_rot.astype(BF16)
             dk_st[slot, :, cols] = dk_acc[:, :nope].astype(BF16)
             dv_st[slot, :, cols] = dv_acc[...].astype(BF16)
+            local, remote = head_copies(g, hh)
+            for copy in remote + local:
+                copy.start()
+            dkv = jnp.concatenate([dk_st[slot, :, cols], dv_st[slot, :, cols]], axis=1)
+            c_s[...] += mm(dkv, wkv_s[h], NT)
             dkr_acc[...] += dk_acc[:, nope:]
             dx_acc[...] += mm(dqt_st[slot, hh * qk:(hh + 1) * qk, chip_cols], wq_s[h, :qk, :], TN)
-        local, remote = pair_copies(g)
-        for copy in local + remote:
-            copy.start()
-        y_acc[...] += mm(ot_st[pl.ds(pl.multiple_of(g * 2 * nope, 2 * nope), 2 * nope), chip_cols], wo_s[slot], TN)
 
         @pl.when(g + 2 < n_pairs)
         def _():
@@ -316,12 +331,11 @@
         return carry
     lax.fori_loop(0, n_pairs, backward, 0)
 
-    theirs = pl.ds(pl.multiple_of((1 - core) * rows, rows), rows)
-    mine = pl.ds(pl.multiple_of(core * rows, rows), rows)
-    sums = [pltpu.make_async_remote_copy(src_ref=acc.at[theirs, :], dst_ref=buf, send_sem=yx_sem.at[idx], recv_sem=yx_sem.at[2 + idx], device_id={'cp': partner}, device_id_type=mesh_id) for idx, (acc, buf) in enumerate(((y_acc, y_buf), (dx_acc, dx_buf)))]
     kr_local = pltpu.make_async_copy(dkr_acc, dkr_out.at[core], kr_sem.at[0])
     kr_remote = pltpu.make_async_remote_copy(src_ref=dkr_acc, dst_ref=dkr_out.at[core], send_sem=kr_sem.at[1], recv_sem=kr_sem.at[2], device_id={'cp': partner}, device_id_type=mesh_id)
-    for copy in sums + [kr_local, kr_remote]:
+    dlat_local = pltpu.make_async_copy(c_s, dlat_out.at[core], dlat_sem.at[0])
+    dlat_remote = pltpu.make_async_remote_copy(src_ref=c_s, dst_ref=dlat_out.at[core], send_sem=dlat_sem.at[1], recv_sem=dlat_sem.at[2], device_id={'cp': partner}, device_id_type=mesh_id)
+    for copy in (dlat_remote, sums[1], kr_remote, kr_local, dlat_local):
         copy.start()
     for arr in range(2):
         for p in range(PARTS):
@@ -330,21 +344,24 @@
                     ring(arr, d, h, p, h == 0).wait_send()
             for rel in range(n_chips):
                 across(arr, rel, p, rel == 0).wait_send()
-    for copy in outs:
+    for copy in (outs[0], outs[1], outs[3]):
         copy.wait()
     ot_local.wait()
     ot_remote.wait()
     for step in range(n_pairs):
-        local, remote = pair_copies(step)
-        if step >= n_pairs - 2:
-            for copy in local:
-                copy.wait()
+        for hh in range(2):
+            local, remote = head_copies(step, hh)
+            if step >= n_pairs - 2:
+                for copy in local:
+                    copy.wait()
+                for copy in remote:
+                    copy.wait_send()
             for copy in remote:
-                copy.wait_send()
-        for copy in remote:
-            copy.wait_recv()
+                copy.wait_recv()
     kr_local.wait()
     kr_remote.wait()
+    dlat_local.wait()
+    dlat_remote.wait()
     for copy in sums:
         copy.wait()
     y_out[...] = (y_acc[mine, :] + y_buf[...]).astype(BF16)
@@ -374,25 +391,25 @@
                vm((seq, 2 * nope), BF16), vm((2 * nope, seq), BF16), vm((seq, 2 * LANES), F32), vm((seq, nope), F32), vm((seq, LANES), F32),
                vm((2 * rows, width), F32), vm((2 * rows, width), F32), vm((rows, width), F32), vm((rows, width), F32),
                vm((2, 2 * qk, seq), BF16), vm((2, seq, 2 * nope), BF16), vm((2, seq, 2 * nope), BF16),
-               dma((2, 2, far, PARTS)), dma((2, 2, far, PARTS)), dma((2, n_chips, PARTS)), dma((2, n_chips, PARTS)), dma((7,)), dma((heads,)), dma((2,)), dma((4,)), dma((2, 3)), dma((2, 3)), dma((n_pairs, 3)), dma((6,)), dma((4,))]
+               dma((2, 2, far, PARTS)), dma((2, 2, far, PARTS)), dma((2, n_chips, PARTS)), dma((2, n_chips, PARTS)), dma((7,)), dma((heads,)), dma((2,)), dma((4,)), dma((2, 2, 3)), dma((2, 2, 3)), dma((n_pairs, 2, 3)), dma((6,)), dma((4,)), dma((3,))]
     return pl.pallas_call(
         functools.partial(block_kernel, n_chips, qk, scale),
-        out_shape=(sds((seq, width), BF16), sds((seq, width), BF16), sds((seq, rank), BF16), sds((seq, rank), F32), sds((n_hv, seq), BF16), sds((n_feat, seq), BF16), sds((seq, n_hv), BF16), sds((seq, n_hv), BF16), sds((2, seq, LANES), F32), sds((rows, width), BF16), sds((rows, width), F32)),
+        out_shape=(sds((seq, width), BF16), sds((seq, width), BF16), sds((seq, rank), BF16), sds((seq, rank), F32), sds((n_hv, seq), BF16), sds((n_feat, seq), BF16), sds((seq, n_hv), BF16), sds((seq, n_hv), BF16), sds((2, seq, LANES), F32), sds((2, seq, rank), F32), sds((rows, width), BF16), sds((rows, width), F32)),
         in_specs=[hbm] * 5 + [vmem] + [hbm] * 4,
-        out_specs=[hbm] * 9 + [vmem] * 2,
+        out_specs=[hbm] * 10 + [vmem] * 2,
         scratch_shapes=scratch,
         compiler_params=pltpu.CompilerParams(collective_id=0, has_side_effects=True, vmem_limit_bytes=67043328),
         name='latent_block',
     )(x_loc, gy_loc, tab, wq_rows, w_dkv, g_row, wkr_t, w_uk, w_uv, wo_rows)
 
 
-def grads_kernel(tile, ot_ref, dqt_ref, gy_ref, x_ref, lat_ref, dk_ref, dv_ref, gwo_ref, gwq_ref, guk_ref, guv_ref,
-                 lhs_s, rhs_s, lat_s, latt_s, kv_s, stage, stage_kv, in_sem, out_sem, kv_sem):
+def grads_kernel(tile, tile_c, chunk, rope_dim, ot_ref, dqt_ref, gy_ref, x_ref, lat_ref, dk_ref, dv_ref, dlat_ref, c_ref, dkr_ref, tab_ref, wdkv_ref, wkr_ref, dxq_ref, gkv_ref, gwo_ref, gwq_ref, guk_ref, guv_ref, gdkv_ref, gkr_ref, gg_ref, dx_ref,
+                 lhs_s, rhs_s, lat_s, latt_s, kv_s, stage, stage_kv, dlat_s, c_s, dkr_s, tab_s, wdkv_s, wkr_s, dxq_s, side_s, sidet_s, dkv_st, in_sem, out_sem, kv_sem, dkv_sem):
     n_o, n_q = ot_ref.shape[0] // tile, dqt_ref.shape[0] // tile
     heads = kv_s.shape[2] // LANES
     rank = lat_s.shape[1]
-    n_c = rank // tile
-    rest = [(ot_ref.at[pl.ds(tile, (n_o - 1) * tile), :], lhs_s.at[pl.ds(tile, (n_o - 1) * tile), :]), (x_ref, rhs_s.at[1]), (dqt_ref, lhs_s.at[pl.ds(n_o * tile, n_q * tile), :]), (lat_ref, lat_s), (dk_ref, kv_s.at[0]), (dv_ref, kv_s.at[1])]
+    n_c = rank // tile_c
+    rest = [(ot_ref.at[pl.ds(tile, (n_o - 1) * tile), :], lhs_s.at[pl.ds(tile, (n_o - 1) * tile), :]), (x_ref, rhs_s.at[1]), (dqt_ref, lhs_s.at[pl.ds(n_o * tile, n_q * tile), :]), (lat_ref, lat_s), (dk_ref, kv_s.at[0]), (dv_ref, kv_s.at[1]), (dlat_ref, dlat_s), (c_ref, c_s), (dkr_ref, dkr_s), (tab_ref, tab_s), (wdkv_ref, wdkv_s), (wkr_ref, wkr_s), (dxq_ref, dxq_s)]
     loads = [pltpu.make_async_copy(src, dst, in_sem.at[idx]) for idx, (src, dst) in enumerate([(ot_ref.at[pl.ds(0, tile), :], lhs_s.at[pl.ds(0, tile), :]), (gy_ref, rhs_s.at[0])] + rest)]
     for copy in loads:
         copy.start()
@@ -437,7 +454,7 @@
 
     def kv_copy(t, dst, base):
         slot = lax.rem(t, 2)
-        size = tile * heads
+        size = tile_c * heads
         return pltpu.make_async_copy(stage_kv.at[slot], dst.at[pl.ds(pl.multiple_of((t - base) * size, size), size), :], kv_sem.at[slot])
 
     def latent_side(t, carry):
@@ -447,10 +464,10 @@
         def _():
             kv_copy(t, guk_ref, t).wait()
         which = jnp.where(t < n_c, 0, 1)
-        row = pl.multiple_of((t - which * n_c) * tile, tile)
-        res = mm(latt_s[pl.ds(row, tile), :], kv_s[which])
+        row = pl.multiple_of((t - which * n_c) * tile_c, tile_c)
+        res = mm(latt_s[pl.ds(row, tile_c), :], kv_s[which])
         for h in range(heads):
-            stage_kv[slot, pl.ds(h, tile, stride=heads), :] = res[:, h * LANES:(h + 1) * LANES]
+            stage_kv[slot, pl.ds(h, tile_c, stride=heads), :] = res[:, h * LANES:(h + 1) * LANES]
 
         @pl.when(t < n_c)
         def _():
@@ -461,31 +478,75 @@
             kv_copy(t, guv_ref, n_c).start()
         return carry
     lax.fori_loop(0, 2 * n_c, latent_side, 0)
+
+    c_raw = c_s[...]
+    inv_rms = lax.rsqrt(jnp.mean(c_raw * c_raw, axis=-1, keepdims=True) + NORM_EPS)
+    c_norm = c_raw * inv_rms
+    d_lat = dlat_s[0] + dlat_s[1]
+    gg_ref[...] = jnp.sum(d_lat * c_norm, axis=0, keepdims=True)
+    d_norm = d_lat * gkv_ref[...]
+    side_s[:, :rank] = (inv_rms * (d_norm - c_norm * jnp.mean(d_norm * c_norm, axis=-1, keepdims=True))).astype(BF16)
+    d_kr = dkr_s[0] + dkr_s[1]
+    tab = tab_s[...]
+    lane = lax.broadcasted_iota(jnp.int32, tab.shape, 1)
+    cos_v = jnp.where(lane < rope_dim, tab, 0.0)
+    sin_v = jnp.where(lane < rope_dim, pltpu.roll(tab, rope_dim, 1), 0.0)
+    side_s[:, rank:] = (d_kr * cos_v - swap_halves(d_kr, rope_dim // 2) * sin_v).astype(BF16)
+    sidet_s[...] = side_s[...].T
+
+    def dkv_copy(t):
+        slot = lax.rem(t, 2)
+        return pltpu.make_async_copy(dkv_st.at[slot], gdkv_ref.at[pl.ds(pl.multiple_of(t * chunk, chunk), chunk), :], dkv_sem.at[slot])
+
+    def side(t, carry):
+        slot = lax.rem(t, 2)
+
+        @pl.when(t >= 2)
+        def _():
+            dkv_copy(t - 2).wait()
+        cols = pl.ds(pl.multiple_of(t * chunk, chunk), chunk)
+        res = mm(sidet_s[...], rhs_s[1, :, cols])
+        dkv_st[slot] = res[:rank, :].T
+        gkr_ref[:, cols] = res[rank:rank + rope_dim, :]
+        dkv_copy(t).start()
+        return carry
+    n_chunks = rhs_s.shape[2] // chunk
+    lax.fori_loop(0, n_chunks, side, 0)
+    rows = dxq_s.shape[0]
+    own = pl.ds(pl.multiple_of(lax.axis_index('cp') * rows, rows), rows)
+    dx_ref[...] = (dxq_s[...] + mm(side_s[own, :rank], wdkv_s[...], NT) + mm(side_s[own, rank:rank + rope_dim], wkr_s[...])).astype(BF16)
+    for t in range(n_chunks - 2, n_chunks):
+        dkv_copy(t).wait()
     for t in range(2):
         out_copy(t, gwo_ref, t).wait()
         kv_copy(t, guk_ref, t).wait()
 
 
-def big_grads(o_t, dq_t, gy_all, x_all, latent, dk, dv):
-    tile = 256
+def big_grads(o_t, dq_t, gy_all, x_all, latent, dk, dv, dlat, c_raw, dkr, tab, w_dkv, wkr_t, dx_q, g_row):
+    tile, tile_c, chunk = 512, 256, 512
     seq, width = x_all.shape
     n_hv, n_feat, rank = o_t.shape[0], dq_t.shape[0], latent.shape[1]
     heads = n_hv // LANES
+    rows = dx_q.shape[0]
+    rope_dim = wkr_t.shape[0]
     hbm = pl.BlockSpec(memory_space=pl.ANY)
+    vmem = pl.BlockSpec(memory_space=pltpu.VMEM)
     dma = pltpu.SemaphoreType.DMA
     vm = pltpu.VMEM
     sds = jax.ShapeDtypeStruct
-    flops = 2 * seq * width * (n_hv + n_feat) + 4 * seq * rank * n_hv
+    flops = 2 * seq * width * (n_hv + n_feat + rank) + 4 * seq * rank * n_hv
     return pl.pallas_call(
-        functools.partial(grads_kernel, tile),
-        out_shape=(sds((n_hv, width), F32), sds((n_feat, width), F32), sds((rank * heads, LANES), F32), sds((rank * heads, LANES), F32)),
-        in_specs=[hbm] * 7,
-        out_specs=[hbm] * 4,
-        scratch_shapes=[vm((n_hv + n_feat, seq), BF16), vm((2, seq, width), BF16), vm((seq, rank), BF16), vm((rank, seq), BF16), vm((2, seq, n_hv), BF16), vm((2, tile, width), F32), vm((2, tile * heads, LANES), F32), dma((8,)), dma((2,)), dma((2,))],
-        compiler_params=pltpu.CompilerParams(vmem_limit_bytes=56 * 1024 * 1024),
-        cost_estimate=pl.CostEstimate(flops=flops, bytes_accessed=80 * 1024 * 1024, transcendentals=0),
+        functools.partial(grads_kernel, tile, tile_c, chunk, rope_dim),
+        out_shape=(sds((n_hv, width), F32), sds((n_feat, width), F32), sds((rank * heads, LANES), F32), sds((rank * heads, LANES), F32), sds((width, rank), F32), sds((rope_dim, width), F32), sds((1, rank), F32), sds((rows, width), BF16)),
+        in_specs=[hbm] * 14 + [vmem],
+        out_specs=[hbm] * 5 + [vmem] * 3,
+        scratch_shapes=[vm((n_hv + n_feat, seq), BF16), vm((2, seq, width), BF16), vm((seq, rank), BF16), vm((rank, seq), BF16), vm((2, seq, n_hv), BF16), vm((2, tile, width), F32), vm((2, tile_c * heads, LANES), F32),
+                        vm((2, seq, rank), F32), vm((seq, rank), F32), vm((2, seq, LANES), F32), vm((seq, LANES), F32), vm((width, rank), BF16), vm((rope_dim, width), BF16), vm((rows, width), F32), vm((seq, rank + LANES), BF16), vm((rank + LANES, seq), BF16), vm((2, chunk, rank), F32),
+                        dma((15,)), dma((2,)), dma((2,)), dma((2,))],
+        compiler_params=pltpu.CompilerParams(vmem_limit_bytes=67043328),
+        cost_estimate=pl.CostEstimate(flops=flops, bytes_accessed=90 * 1024 * 1024, transcendentals=0),
         name='weight_grads',
-    )(o_t, dq_t, gy_all, x_all, latent, dk, dv)
+    )(o_t, dq_t, gy_all, x_all, latent, dk, dv, dlat, c_raw, dkr, tab, w_dkv, wkr_t, dx_q, g_row)
 
 
 def solution(mesh):
@@ -502,7 +563,6 @@
         rank = w_dkv.shape[1]
         nope = qk - rope_dim
         scale = qk ** -0.5
-        me = lax.axis_index('cp')
         half = rope_dim // 2
         inv_freq = ROPE_THETA ** (-(np.arange(half) * 2.0 / rope_dim))
         angles = np.arange(seq)[:, None] * inv_freq[None, :]
@@ -511,30 +571,12 @@
 
         wq_rows = jnp.transpose(w_q, (1, 2, 0)).reshape(heads * qk, width)
         wo_rows = w_o.reshape(heads * nope, width)
-        wuk_cols = w_uk.reshape(rank, heads * nope)
-        wuv_cols = w_uv.reshape(rank, heads * nope)
         g_f32 = g_kv.astype(F32)
-        x_all, gy_all, latent, c_raw, o_t, dq_t, dk, dv, dkr, y_loc, dx_q = block(x_loc, gy_loc, tab, wq_rows, w_dkv, g_f32[None, :], w_kr.T, w_uk, w_uv, wo_rows, n_dev, qk, scale)
-        inv_rms = lax.rsqrt(jnp.mean(c_raw * c_raw, axis=-1, keepdims=True) + NORM_EPS)
-        c_norm = c_raw * inv_rms
-
-        own = lambda t: lax.dynamic_slice_in_dim(t, me * rows, rows, 0)
-        tn = lambda a, b: lax.dot_general(a, b, (((0,), (0,)), ((), ())), preferred_element_type=F32)
-        gwo, gwq, guk, guv = big_grads(o_t, dq_t, gy_all, x_all, latent, dk, dv)
-        gw_o = gwo.reshape(w_o.shape)
+        g_row = g_f32[None, :]
+        wkr_t = w_kr.T
+        x_all, gy_all, latent, c_raw, o_t, dq_t, dk, dv, dkr, dlat, y_loc, dx_q = block(x_loc, gy_loc, tab, wq_rows, w_dkv, g_row, wkr_t, w_uk, w_uv, wo_rows, n_dev, qk, scale)
+        gwo, gwq, guk, guv, gw_dkv, gkr_t, gg, dx_loc = big_grads(o_t, dq_t, gy_all, x_all, latent, dk, dv, dlat, c_raw, dkr, tab, w_dkv, wkr_t, dx_q, g_row)
         gw_q = jnp.transpose(gwq.reshape(heads, qk, width), (2, 0, 1))
-        gw_uk, gw_uv = guk.reshape(w_uk.shape), guv.reshape(w_uv.shape)
-        d_latent = mm(dk, wuk_cols, NT) + mm(dv, wuv_cols, NT)
-        gg_kv = jnp.sum(d_latent * c_norm, axis=0)
-        d_norm = d_latent * g_f32
-        dc_raw = (inv_rms * (d_norm - c_norm * jnp.mean(d_norm * c_norm, axis=-1, keepdims=True))).astype(BF16)
-        d_kr = (dkr[0] + dkr[1])[:, :rope_dim]
-        r1, r2 = d_kr[:, :half], d_kr[:, half:]
-        cos, sin = tab[:, :half], tab[:, LANES - half:]
-        dkr_raw = jnp.concatenate([r1 * cos + r2 * sin, r2 * cos - r1 * sin], axis=1).astype(BF16)
-        gw_dkv = tn(x_all, dc_raw)
-        gw_kr = tn(dkr_raw, x_all).T
-        dx_loc = dx_q + mm(own(dc_raw), w_dkv, NT) + mm(own(dkr_raw), w_kr, NT)
-        return (y_loc, dx_loc.astype(BF16), gw_q, gw_dkv, gg_kv, gw_kr, gw_uk, gw_uv, gw_o)
+        return (y_loc, dx_loc, gw_q, gw_dkv, gg.reshape(rank), gkr_t.T, guk.reshape(w_uk.shape), guv.reshape(w_uv.shape), gwo.reshape(w_o.shape))
 
     return jax.shard_map(device_fn, mesh=mesh, in_specs=in_specs, out_specs=out_specs, check_vma=False)

time: 167 us -> 157 us (0.940)
  matrix products: 17.1 us -> 0 us
  Pallas kernels: 142 us -> 153 us
  other arithmetic: 3.98 us -> 1.26 us
    dot_general x6 -> x0, matrix products: 17.1 us -> none  [the longest x4 11 us: mm(): return lax.dot_general(lhs, rhs, dims, preferred_element_type=F32)]
    pallas_call x1, Pallas kernels: 106 us -> 111 us  [block(): pl.pallas_call(functools.partial(block_kernel, n_chips, qk, scale), out_s...]
    pallas_call x1, Pallas kernels: 36.4 us -> 41.4 us  [big_grads(): pl.pallas_call(functools.partial(grads_kernel, tile, tile_c, chunk, rope_...]
    reduce_sum x1 -> x0, other arithmetic: 1.96 us -> none  [device_fn(): jnp.mean(c_raw * c_raw, axis=-1, keepdims=True) + NORM_EPS]
    convert_element_type x2 -> x0, other arithmetic: 1.7 us -> none  [the longest x1 1.26 us: device_fn(): g_f32 = g_kv.astype(F32)]
where the time goes in v3:
time: 157 us; the launch traced here: 156 us
  Pallas kernels  153 us (97%)
  local copies, waits for them, and re-layouts  1.67 us (1%)
    pallas_call x1, Pallas kernels, block(): pl.pallas_call(functools.partial(block_kernel, n_chips, qk, scale), out_s...  111 us
    pallas_call x1, Pallas kernels, big_grads(): pl.pallas_call(functools.partial(grads_kernel, tile, tile_c, chunk, rope_...  41.4 us

profile of v3, /device:TPU:21, one launch (start us, length us, event | category | flops | bytes accessed | tf_op | source)
XLA Modules:
  0.0 156.4 jit_solution(8714999489618845390)
XLA Ops:
  0.6 1.3 broadcast_in_dim.7
  1.9 111.4 %latent_block.1 = (bf16[1024,2048]{1,0:T(8,128)(2,1)}, bf16[1024,2048]{1,0:T(8,128)(2,1)}, bf16[1024,512]{1,0:T(8,128)(2,1)}, f32[1024,512]{1,0:T(8,128)}, bf16[...) custom-call(bf16[64,2048]{1,0:T(8,128)(2,1)} %x_ref.1, ...), custom_call_target="tpu_custom_call" | custom-call | tf_op jit(solution)/shard_map/latent_block/pallas_call | solution.py:395
  113.3 41.4 %weight_grads.1 = (f32[2048,2048]{1,0:T(8,128)}, f32[3072,2048]{1,0:T(8,128)}, f32[8192,128]{1,0:T(8,128)}, f32[8192,128]{1,0:T(8,128)}, f32[2048,512]{1,0:T(8,1...) custom-call(bf16[2048,1024]{1,0:T(8,128)(2,1)} %get-tuple-element.30.ot_ref, ...), custom_call_target="tpu_custom_call" | custom-call | flops 27917287424 | bytes 94371840 | tf_op jit(solution)/shard_map/weight_grads/pallas_call | solution.py:538
  154.7 1.7 %copy.20 = bf16[64,2048]{1,0:T(8,128)(2,1)} copy(bf16[64,2048]{1,0:T(8,128)(2,1)} %get-tuple-element.58) | data formatting | bytes 524288

commit v4 on v3

--- a/solution.py
+++ b/solution.py
@@ -403,15 +403,15 @@
     )(x_loc, gy_loc, tab, wq_rows, w_dkv, g_row, wkr_t, w_uk, w_uv, wo_rows)
 
 
-def grads_kernel(tile, tile_c, chunk, rope_dim, ot_ref, dqt_ref, gy_ref, x_ref, lat_ref, dk_ref, dv_ref, dlat_ref, c_ref, dkr_ref, tab_ref, wdkv_ref, wkr_ref, dxq_ref, gkv_ref, gwo_ref, gwq_ref, guk_ref, guv_ref, gdkv_ref, gkr_ref, gg_ref, dx_ref,
-                 lhs_s, rhs_s, lat_s, latt_s, kv_s, stage, stage_kv, dlat_s, c_s, dkr_s, tab_s, wdkv_s, wkr_s, dxq_s, side_s, sidet_s, dkv_st, in_sem, out_sem, kv_sem, dkv_sem):
+def grads_kernel(tile, tile_c, chunk, rope_dim, ot_ref, dqt_ref, gy_ref, x_ref, lat_ref, dk_ref, dv_ref, dlat_ref, c_ref, dkr_ref, tab_ref, wdkv_ref, wkr_ref, dxq_ref, yin_ref, gkv_ref, gwo_ref, gwq_ref, guk_ref, guv_ref, gdkv_ref, y_ref, gkr_ref, gg_ref, dx_ref,
+                 lhs_s, rhs_s, lat_s, latt_s, kv_s, stage, stage_kv, dlat_s, c_s, dkr_s, tab_s, wdkv_s, wkr_s, dxq_s, y_s, side_s, sidet_s, dkv_st, in_sem, out_sem, kv_sem, dkv_sem, y_sem):
     n_o, n_q = ot_ref.shape[0] // tile, dqt_ref.shape[0] // tile
     heads = kv_s.shape[2] // LANES
     rank = lat_s.shape[1]
     n_c = rank // tile_c
-    rest = [(ot_ref.at[pl.ds(tile, (n_o - 1) * tile), :], lhs_s.at[pl.ds(tile, (n_o - 1) * tile), :]), (x_ref, rhs_s.at[1]), (dqt_ref, lhs_s.at[pl.ds(n_o * tile, n_q * tile), :]), (lat_ref, lat_s), (dk_ref, kv_s.at[0]), (dv_ref, kv_s.at[1]), (dlat_ref, dlat_s), (c_ref, c_s), (dkr_ref, dkr_s), (tab_ref, tab_s), (wdkv_ref, wdkv_s), (wkr_ref, wkr_s), (dxq_ref, dxq_s)]
+    rest = [(ot_ref.at[pl.ds(tile, (n_o - 1) * tile), :], lhs_s.at[pl.ds(tile, (n_o - 1) * tile), :]), (x_ref, rhs_s.at[1]), (dqt_ref, lhs_s.at[pl.ds(n_o * tile, n_q * tile), :]), (lat_ref, lat_s), (dk_ref, kv_s.at[0]), (dv_ref, kv_s.at[1]), (dlat_ref, dlat_s), (c_ref, c_s), (dkr_ref, dkr_s), (tab_ref, tab_s), (wdkv_ref, wdkv_s), (wkr_ref, wkr_s), (dxq_ref, dxq_s), (yin_ref, y_s)]
     loads = [pltpu.make_async_copy(src, dst, in_sem.at[idx]) for idx, (src, dst) in enumerate([(ot_ref.at[pl.ds(0, tile), :], lhs_s.at[pl.ds(0, tile), :]), (gy_ref, rhs_s.at[0])] + rest)]
-    for copy in loads:
+    for copy in loads[:2]:
         copy.start()
 
     def out_copy(t, dst, base):
@@ -420,6 +420,7 @@
 
     loads[0].wait()
     loads[1].wait()
+    loads[2].start()
 
     def product(t, carry):
         slot = lax.rem(t, 2)
@@ -427,6 +428,8 @@
         @pl.when(t == 1)
         def _():
             loads[2].wait()
+            for copy in loads[3:]:
+                copy.start()
 
         @pl.when(t == n_o)
         def _():
@@ -451,6 +454,8 @@
     for copy in loads[5:]:
         copy.wait()
     latt_s[...] = lat_s[...].T
+    y_copy = pltpu.make_async_copy(y_s, y_ref, y_sem.at[0])
+    y_copy.start()
 
     def kv_copy(t, dst, base):
         slot = lax.rem(t, 2)
@@ -517,12 +522,13 @@
     dx_ref[...] = (dxq_s[...] + mm(side_s[own, :rank], wdkv_s[...], NT) + mm(side_s[own, rank:rank + rope_dim], wkr_s[...])).astype(BF16)
     for t in range(n_chunks - 2, n_chunks):
         dkv_copy(t).wait()
+    y_copy.wait()
     for t in range(2):
         out_copy(t, gwo_ref, t).wait()
         kv_copy(t, guk_ref, t).wait()
 
 
-def big_grads(o_t, dq_t, gy_all, x_all, latent, dk, dv, dlat, c_raw, dkr, tab, w_dkv, wkr_t, dx_q, g_row):
+def big_grads(o_t, dq_t, gy_all, x_all, latent, dk, dv, dlat, c_raw, dkr, tab, w_dkv, wkr_t, dx_q, y_in, g_row):
     tile, tile_c, chunk = 512, 256, 512
     seq, width = x_all.shape
     n_hv, n_feat, rank = o_t.shape[0], dq_t.shape[0], latent.shape[1]
@@ -537,16 +543,16 @@
     flops = 2 * seq * width * (n_hv + n_feat + rank) + 4 * seq * rank * n_hv
     return pl.pallas_call(
         functools.partial(grads_kernel, tile, tile_c, chunk, rope_dim),
-        out_shape=(sds((n_hv, width), F32), sds((n_feat, width), F32), sds((rank * heads, LANES), F32), sds((rank * heads, LANES), F32), sds((width, rank), F32), sds((rope_dim, width), F32), sds((1, rank), F32), sds((rows, width), BF16)),
-        in_specs=[hbm] * 14 + [vmem],
-        out_specs=[hbm] * 5 + [vmem] * 3,
+        out_shape=(sds((n_hv, width), F32), sds((n_feat, width), F32), sds((rank * heads, LANES), F32), sds((rank * heads, LANES), F32), sds((width, rank), F32), sds((rows, width), BF16), sds((rope_dim, width), F32), sds((1, rank), F32), sds((rows, width), BF16)),
+        in_specs=[hbm] * 15 + [vmem],
+        out_specs=[hbm] * 6 + [vmem] * 3,
         scratch_shapes=[vm((n_hv + n_feat, seq), BF16), vm((2, seq, width), BF16), vm((seq, rank), BF16), vm((rank, seq), BF16), vm((2, seq, n_hv), BF16), vm((2, tile, width), F32), vm((2, tile_c * heads, LANES), F32),
-                        vm((2, seq, rank), F32), vm((seq, rank), F32), vm((2, seq, LANES), F32), vm((seq, LANES), F32), vm((width, rank), BF16), vm((rope_dim, width), BF16), vm((rows, width), F32), vm((seq, rank + LANES), BF16), vm((rank + LANES, seq), BF16), vm((2, chunk, rank), F32),
-                        dma((15,)), dma((2,)), dma((2,)), dma((2,))],
+                        vm((2, seq, rank), F32), vm((seq, rank), F32), vm((2, seq, LANES), F32), vm((seq, LANES), F32), vm((width, rank), BF16), vm((rope_dim, width), BF16), vm((rows, width), F32), vm((rows, width), BF16), vm((seq, rank + LANES), BF16), vm((rank + LANES, seq), BF16), vm((2, chunk, rank), F32),
+                        dma((16,)), dma((2,)), dma((2,)), dma((2,)), dma((1,))],
         compiler_params=pltpu.CompilerParams(vmem_limit_bytes=67043328),
         cost_estimate=pl.CostEstimate(flops=flops, bytes_accessed=90 * 1024 * 1024, transcendentals=0),
         name='weight_grads',
-    )(o_t, dq_t, gy_all, x_all, latent, dk, dv, dlat, c_raw, dkr, tab, w_dkv, wkr_t, dx_q, g_row)
+    )(o_t, dq_t, gy_all, x_all, latent, dk, dv, dlat, c_raw, dkr, tab, w_dkv, wkr_t, dx_q, y_in, g_row)
 
 
 def solution(mesh):
@@ -574,8 +580,8 @@
         g_f32 = g_kv.astype(F32)
         g_row = g_f32[None, :]
         wkr_t = w_kr.T
-        x_all, gy_all, latent, c_raw, o_t, dq_t, dk, dv, dkr, dlat, y_loc, dx_q = block(x_loc, gy_loc, tab, wq_rows, w_dkv, g_row, wkr_t, w_uk, w_uv, wo_rows, n_dev, qk, scale)
-        gwo, gwq, guk, guv, gw_dkv, gkr_t, gg, dx_loc = big_grads(o_t, dq_t, gy_all, x_all, latent, dk, dv, dlat, c_raw, dkr, tab, w_dkv, wkr_t, dx_q, g_row)
+        x_all, gy_all, latent, c_raw, o_t, dq_t, dk, dv, dkr, dlat, y_in, dx_q = block(x_loc, gy_loc, tab, wq_rows, w_dkv, g_row, wkr_t, w_uk, w_uv, wo_rows, n_dev, qk, scale)
+        gwo, gwq, guk, guv, gw_dkv, y_loc, gkr_t, gg, dx_loc = big_grads(o_t, dq_t, gy_all, x_all, latent, dk, dv, dlat, c_raw, dkr, tab, w_dkv, wkr_t, dx_q, y_in, g_row)
         gw_q = jnp.transpose(gwq.reshape(heads, qk, width), (2, 0, 1))
         return (y_loc, dx_loc, gw_q, gw_dkv, gg.reshape(rank), gkr_t.T, guk.reshape(w_uk.shape), guv.reshape(w_uv.shape), gwo.reshape(w_o.shape))
 

time: 157 us -> 158 us (level)
  Pallas kernels: 153 us -> 156 us
  local copies, waits for them, and re-layouts: 1.67 us -> 0 us
    pallas_call x1, Pallas kernels: 41.4 us -> 44.4 us  [big_grads(): pl.pallas_call(functools.partial(grads_kernel, tile, tile_c, chunk, rope_...]
    unnamed x1 -> x0, local copies, waits for them, and re-layouts: 1.67 us -> none
where the time goes in v4:
time: 158 us
  Pallas kernels  156 us (99%)
    pallas_call x1, Pallas kernels, block(): pl.pallas_call(functools.partial(block_kernel, n_chips, qk, scale), out_s...  111 us
    pallas_call x1, Pallas kernels, big_grads(): pl.pallas_call(functools.partial(grads_kernel, tile, tile_c, chunk, rope_...  44.4 us

profile of v4, /device:TPU:21, one launch (start us, length us, event | category | flops | bytes accessed | tf_op | source)
XLA Modules:
  0.0 157.8 jit_solution(14937405258651684519)
XLA Ops:
  0.6 1.3 broadcast_in_dim.7
  1.9 111.4 %latent_block.1 = (bf16[1024,2048]{1,0:T(8,128)(2,1)}, bf16[1024,2048]{1,0:T(8,128)(2,1)}, bf16[1024,512]{1,0:T(8,128)(2,1)}, f32[1024,512]{1,0:T(8,128)}, bf16[...) custom-call(bf16[64,2048]{1,0:T(8,128)(2,1)} %x_ref.1, ...), custom_call_target="tpu_custom_call" | custom-call | tf_op jit(solution)/shard_map/latent_block/pallas_call | solution.py:395
  113.3 44.4 %weight_grads.1 = (f32[2048,2048]{1,0:T(8,128)}, f32[3072,2048]{1,0:T(8,128)}, f32[8192,128]{1,0:T(8,128)}, f32[8192,128]{1,0:T(8,128)}, f32[2048,512]{1,0:T(8,1...) custom-call(bf16[2048,1024]{1,0:T(8,128)(2,1)} %get-tuple-element.30.ot_ref, ...), custom_call_target="tpu_custom_call" | custom-call | flops 27917287424 | bytes 94371840 | tf_op jit(solution)/shard_map/weight_grads/pallas_call | solution.py:544
